TPU v7x, 256 devices: a whole 4x4x8 slice. The times are simulated.
256 devices in a mesh: grp: 2 (over core), dom: 128 (over y, x, z).
Axes of the slice: x: 4, y: 4, z: 8, core: 2. Of those that a mesh axis runs over, the one named last changes fastest.
Arguments:
- node_latent: bfloat16 [262144, 128], P(('grp', 'dom')), may hold values from -6 to 6
- edge_latent: bfloat16 [1572864, 128], P(('grp', 'dom')), may hold values from -6 to 6
- mig_send: int32 [256, 256], P(('grp', 'dom')), may hold values from 0 to 1024, as said below
- mig_recv: int32 [262144], P(('grp', 'dom')), may hold values from 0 to 1279, as said below
- halo_send: int32 [256, 128], P(('grp', 'dom')), may hold values from 0 to 1024, as said below
- cross_send: int32 [256, 32], P(('grp', 'dom')), may hold values from 0 to 1024, as said below
- senders: int32 [1572864], P(('grp', 'dom')), may hold values from 0 to 1183, as said below
- receivers: int32 [1572864], P(('grp', 'dom')), may hold values from 0 to 1023
- edge_live: int32 [1572864], P(('grp', 'dom')), may hold values from 0 to 1, as said below
- edge_w1: bfloat16 [384, 128], replicated, may hold values from -0.3125 to 0.3125
- edge_b1: float32 [128], replicated, may hold values from -2 to 2
- edge_w2: bfloat16 [128, 128], replicated, may hold values from -0.5 to 0.5
- edge_b2: float32 [128], replicated, may hold values from -2 to 2
- edge_gain: float32 [128], replicated, may hold values from 0.25 to 1.75
- edge_bias: float32 [128], replicated, may hold values from -2 to 2
- node_w1: bfloat16 [256, 128], replicated, may hold values from -0.375 to 0.375
- node_b1: float32 [128], replicated, may hold values from -2 to 2
- node_w2: bfloat16 [128, 128], replicated, may hold values from -0.5 to 0.5
- node_b2: float32 [128], replicated, may hold values from -2 to 2
- node_gain: float32 [128], replicated, may hold values from 0.25 to 1.75
- node_bias: float32 [128], replicated, may hold values from -2 to 2
Outputs:
- node_out: bfloat16 [262144, 128], P(('grp', 'dom'))
- edge_out: bfloat16 [1572864, 128], P(('grp', 'dom'))
Inputs may be any that keep to these rules, and one draw needn't show every extreme that they name: `mig_send`: per partition, slot k * 64 + c names an old local row moving to the partition at distance o_k, or 1024 for an empty slot; live slots of one distance come first, every old row is named at most once, and a partition sends to a partition exactly as many rows as it receives from it. Where the peer exists, 32 or more slots of a distance are live; slots toward missing partitions are empty; in every draw some partition of each region fills all its slots both ways. `mig_recv`: for each partition, 1024 distinct entries of its source table: old rows it did not send and live arrived slots, each exactly once. `halo_send`: slot k * 32 + c names a new local row sent to the partition at distance o_k, or 1024 if empty; live slots come first, rows are distinct within a partition; where the peer exists 32 // 2 or more are live, and some partition of each region fills all slots whose peer exists. `cross_send`: new local rows sent to the same partition of the other region, or 1024 if empty; live slots come first, 16 or more live, distinct from that partition's halo_send rows; some partition of each region fills all. `senders`: each entry names a new local row (below 1024) or a live halo or cross slot of the extended table. `edge_live`: within a partition, the live edge slots are a prefix of at least 3072 slots; some partition is fully live in every draw.
All inputs are finite; a program needn't handle non-finite values.
Results may differ from a plain program's by a relative error of at most 0.0075.
Values may be sent and summed in bfloat16 or wider, within the bound.
A program may use at most 64 MiB of HBM per device.

v0:
```python
import jax
import jax.numpy as jnp
from jax import lax
from jax.sharding import PartitionSpec as P

R = 2
TILE = 128


EPSILON = 1e-05


def passed_along(value, axis, steps):
    count = lax.axis_size(axis)
    first, last = (max(0, -steps), min(count, count - steps))
    return lax.ppermute(value, axis, [(source, source + steps) for source in range(first, last)])


def swapped(value, axis, distance):
    return lax.ppermute(value, axis, [(i, i ^ 1 << distance) for i in range(lax.axis_size(axis))])


def offset_list():
    return [number - R if number < R else number - R + 1 for number in range(2 * R)]


def layer_norm(values, scale_vec, offset_vec):
    center = values - jnp.mean(values, axis=-1, keepdims=True)
    spread = jnp.mean(center * center, axis=-1, keepdims=True)
    return center * lax.rsqrt(spread + EPSILON) * scale_vec + offset_vec


def select_rows(source_rows, wanted):
    marks = (wanted[:, None] == jnp.arange(source_rows.shape[0], dtype=jnp.int32)[None, :]).astype(
        jnp.bfloat16
    )
    return jnp.dot(marks, source_rows, preferred_element_type=jnp.float32).astype(jnp.bfloat16)


def body(
    node_latent,
    edge_latent,
    mig_send,
    mig_recv,
    halo_send,
    cross_send,
    senders,
    receivers,
    edge_live,
    edge_w1,
    edge_b1,
    edge_w2,
    edge_b2,
    edge_gain,
    edge_bias,
    node_w1,
    node_b1,
    node_w2,
    node_b2,
    node_gain,
    node_bias,
):
    latent = node_latent.shape[1]
    node_count = node_latent.shape[0]
    distances = 2 * R
    move_slots = mig_send.shape[1] // distances
    halo_slots = halo_send.shape[1] // distances
    leaving = select_rows(node_latent, mig_send.reshape(-1)).reshape(distances, move_slots, latent)
    arrived = jnp.concatenate(
        [passed_along(leaving[place], "dom", shift) for place, shift in enumerate(offset_list())],
        axis=0,
    )
    source_rows = jnp.concatenate([node_latent, arrived], axis=0)
    fresh = select_rows(source_rows, mig_recv)
    halo_out = select_rows(fresh, halo_send.reshape(-1)).reshape(distances, halo_slots, latent)
    halo_in = jnp.concatenate(
        [passed_along(halo_out[place], "dom", shift) for place, shift in enumerate(offset_list())],
        axis=0,
    )
    cross_in = swapped(select_rows(fresh, cross_send.reshape(-1)), "grp", 0)
    extended = jnp.concatenate([fresh, halo_in, cross_in], axis=0)
    block_rows = 4 * TILE
    blocks = edge_latent.shape[0] // block_rows
    node_ids = jnp.arange(node_count, dtype=jnp.int32)

    def edge_block(inbound, pieces):
        edge_rows, sender_ids, receiver_ids, active = pieces
        sent_side = select_rows(extended, sender_ids)
        marks = (receiver_ids[:, None] == node_ids[None, :]).astype(jnp.bfloat16)
        recv_side = jnp.dot(marks, fresh, preferred_element_type=jnp.float32).astype(jnp.bfloat16)
        joined = jnp.concatenate([edge_rows, sent_side, recv_side], axis=1)
        hidden = jnp.maximum(
            jnp.dot(joined, edge_w1, preferred_element_type=jnp.float32) + edge_b1, 0.0
        ).astype(jnp.bfloat16)
        before = jnp.dot(hidden, edge_w2, preferred_element_type=jnp.float32) + edge_b2
        message = layer_norm(before, edge_gain, edge_bias).astype(jnp.bfloat16)
        kept = message * active.astype(jnp.bfloat16)[:, None]
        inbound = inbound + lax.dot_general(
            marks, kept, (((0,), (0,)), ((), ())), preferred_element_type=jnp.float32
        )
        updated = (edge_rows.astype(jnp.float32) + kept.astype(jnp.float32)).astype(jnp.bfloat16)
        return (inbound, updated)

    inbound, updated = lax.scan(
        edge_block,
        jnp.zeros((node_count, latent), jnp.float32),
        (
            edge_latent.reshape(blocks, block_rows, latent),
            senders.reshape(blocks, block_rows),
            receivers.reshape(blocks, block_rows),
            edge_live.reshape(blocks, block_rows),
        ),
    )
    node_in = jnp.concatenate([fresh, inbound.astype(jnp.bfloat16)], axis=1)
    node_hidden = jnp.maximum(
        jnp.dot(node_in, node_w1, preferred_element_type=jnp.float32) + node_b1, 0.0
    ).astype(jnp.bfloat16)
    node_before = jnp.dot(node_hidden, node_w2, preferred_element_type=jnp.float32) + node_b2
    node_out = (fresh.astype(jnp.float32) + layer_norm(node_before, node_gain, node_bias)).astype(
        jnp.bfloat16
    )
    return (node_out, updated.reshape(-1, latent))


def solution(mesh):
    placed = (
        P(("grp", "dom"), None),
        P(("grp", "dom"), None),
        P(("grp", "dom"), None),
        P(("grp", "dom")),
        P(("grp", "dom"), None),
        P(("grp", "dom"), None),
        P(("grp", "dom")),
        P(("grp", "dom")),
        P(("grp", "dom")),
        P(),
        P(),
        P(),
        P(),
        P(),
        P(),
        P(),
        P(),
        P(),
        P(),
        P(),
        P(),
    )
    return jax.shard_map(
        body,
        mesh=mesh,
        in_specs=placed,
        out_specs=(P(("grp", "dom"), None), P(("grp", "dom"), None)),
        check_vma=False,
    )
```

profile of v0, /device:TPU:24, one launch (start us, length us, event | category | flops | bytes accessed | tf_op | source)
XLA Modules:
  0.0 106.8 jit_solution(18043968294181258914)
XLA Ops:
  0.7 1.4 %convolution_convert_fusion = bf16[256,128]{1,0:T(8,128)(2,1)S(1)} fusion(bf16[1024,128]{1,0:T(8,128)(2,1)} %param.23, s32[256]{0:T(256)} %bitcast.45), kind=kOutput, calls=%fused_computation.45 | convolution fusion | flops 67403776 | bytes 328704 | tf_op jit(solution)/shard_map/dot_general | solution.py:37
  2.0 5.2 %collective-permute-start.3 = (bf16[64,128]{1,0:T(8,128)(2,1)S(1)}, bf16[64,128]{1,0:T(8,128)(2,1)S(1)}, u32[]{:S(2)}, u32[]{:S(2)}) collective-permute-start(bf16[64,128]{1,0:T(8,128)(2,1)S(1)} %get-tuple-element.186), channel_id=1, source_target_pairs={{0,2},{1,3},{2,4},{3,5},{4,6},{5,7},{6,8},{7,9},{8,10},{9,11},{10,... | collective-permute-start | bytes 49160 | tf_op jit(solution)/shard_map/ppermute | solution.py:16
  7.2 3.8 %collective-permute-start.2 = (bf16[64,128]{1,0:T(8,128)(2,1)S(1)}, bf16[64,128]{1,0:T(8,128)(2,1)S(1)}, u32[]{:S(2)}, u32[]{:S(2)}) collective-permute-start(bf16[64,128]{1,0:T(8,128)(2,1)S(1)} %get-tuple-element.187), channel_id=1, source_target_pairs={{0,1},{1,2},{2,3},{3,4},{4,5},{5,6},{6,7},{7,8},{8,9},{9,10},{10,1... | collective-permute-start | bytes 49160 | tf_op jit(solution)/shard_map/ppermute | solution.py:16
  11.1 6.2 %collective-permute-start.1 = (bf16[64,128]{1,0:T(8,128)(2,1)S(1)}, bf16[64,128]{1,0:T(8,128)(2,1)S(1)}, u32[]{:S(2)}, u32[]{:S(2)}) collective-permute-start(bf16[64,128]{1,0:T(8,128)(2,1)S(1)} %get-tuple-element.188), channel_id=1, source_target_pairs={{1,0},{2,1},{3,2},{4,3},{5,4},{6,5},{7,6},{8,7},{9,8},{10,9},{11,1... | collective-permute-start | bytes 49160 | tf_op jit(solution)/shard_map/ppermute | solution.py:16
  17.3 3.6 %collective-permute-start = (bf16[64,128]{1,0:T(8,128)(2,1)S(1)}, bf16[64,128]{1,0:T(8,128)(2,1)S(1)}, u32[]{:S(2)}, u32[]{:S(2)}) collective-permute-start(bf16[64,128]{1,0:T(8,128)(2,1)S(1)} %get-tuple-element.189), channel_id=1, source_target_pairs={{2,0},{3,1},{4,2},{5,3},{6,4},{7,5},{8,6},{9,7},{10,8},{11,9},{12,... | collective-permute-start | bytes 49160 | tf_op jit(solution)/shard_map/ppermute | solution.py:16
  20.9 1.0 constant_dynamic-update-slice_fusion.5
  24.3 1.0 constant_dynamic-update-slice_fusion.11
  25.6 7.7 %collective-permute-start.4 = (bf16[32,128]{1,0:T(8,128)(2,1)S(1)}, bf16[32,128]{1,0:T(8,128)(2,1)S(1)}, u32[]{:S(2)}, u32[]{:S(2)}) collective-permute-start(bf16[32,128]{1,0:T(8,128)(2,1)S(1)} %get-tuple-element.193), channel_id=1, source_target_pairs={{2,0},{3,1},{4,2},{5,3},{6,4},{7,5},{8,6},{9,7},{10,8},{11,9},{12,... | collective-permute-start | bytes 24584 | tf_op jit(solution)/shard_map/ppermute | solution.py:16
  33.6 1.9 %collective-permute-start.7 = (bf16[32,128]{1,0:T(8,128)(2,1)S(1)}, bf16[32,128]{1,0:T(8,128)(2,1)S(1)}, u32[]{:S(2)}, u32[]{:S(2)}) collective-permute-start(bf16[32,128]{1,0:T(8,128)(2,1)S(1)} %get-tuple-element.190), channel_id=1, source_target_pairs={{0,2},{1,3},{2,4},{3,5},{4,6},{5,7},{6,8},{7,9},{8,10},{9,11},{10,... | collective-permute-start | bytes 24584 | tf_op jit(solution)/shard_map/ppermute | solution.py:16
  35.5 2.3 %collective-permute-start.6 = (bf16[32,128]{1,0:T(8,128)(2,1)S(1)}, bf16[32,128]{1,0:T(8,128)(2,1)S(1)}, u32[]{:S(2)}, u32[]{:S(2)}) collective-permute-start(bf16[32,128]{1,0:T(8,128)(2,1)S(1)} %get-tuple-element.191), channel_id=1, source_target_pairs={{0,1},{1,2},{2,3},{3,4},{4,5},{5,6},{6,7},{7,8},{8,9},{9,10},{10,1... | collective-permute-start | bytes 24584 | tf_op jit(solution)/shard_map/ppermute | solution.py:16
  37.9 7.7 %collective-permute-start.5 = (bf16[32,128]{1,0:T(8,128)(2,1)S(1)}, bf16[32,128]{1,0:T(8,128)(2,1)S(1)}, u32[]{:S(2)}, u32[]{:S(2)}) collective-permute-start(bf16[32,128]{1,0:T(8,128)(2,1)S(1)} %get-tuple-element.192), channel_id=1, source_target_pairs={{1,0},{2,1},{3,2},{4,3},{5,4},{6,5},{7,6},{8,7},{9,8},{10,9},{11,1... | collective-permute-start | bytes 24584 | tf_op jit(solution)/shard_map/ppermute | solution.py:16
  45.6 1.3 %collective-permute-done.5 = bf16[32,128]{1,0:T(8,128)(2,1)S(1)} collective-permute-done((bf16[32,128]{1,0:T(8,128)(2,1)S(1)}, bf16[32,128]{1,0:T(8,128)(2,1)S(1)}, u32[]{:S(2)}, u32[]{:S(2)}) %collective-permute-start.5) | collective-permute-done | bytes 8224 | tf_op jit(solution)/shard_map/ppermute | solution.py:16
  47.1 57.5 %while.13 = (s32[]{:T(128)}, f32[1024,128]{1,0:T(8,128)S(1)}, bf16[12,512,128]{2,1,0:T(8,128)(2,1)}, s32[12,512]{1,0:T(8,128)S(1)}, bf16[12,512,128]{2,1,0:T(8,1...) while((s32[]{:T(128)}, f32[1024,128]{1,0:T(8,128)S(1)}, ...), condition=%wide.region_3.4_spmd.clone, body=%wide.region_0.3_spmd.clone.sunk | while | flops 496059392 | bytes 4804799 | solution.py:104
  48.6 0.9 constant_dynamic-slice_fusion.6
  50.4 0.8 convolution_add_fusion.6
  53.4 0.9 constant_dynamic-slice_fusion.6
  55.2 0.8 convolution_add_fusion.6
  58.2 0.9 constant_dynamic-slice_fusion.6
  60.0 0.8 convolution_add_fusion.6
  63.0 0.9 constant_dynamic-slice_fusion.6
  64.8 0.8 convolution_add_fusion.6
  67.7 0.9 constant_dynamic-slice_fusion.6
  72.5 0.9 constant_dynamic-slice_fusion.6
  77.3 0.9 constant_dynamic-slice_fusion.6
  82.1 0.9 constant_dynamic-slice_fusion.6
  86.9 0.9 constant_dynamic-slice_fusion.6
  91.7 0.9 constant_dynamic-slice_fusion.6
  96.5 0.9 constant_dynamic-slice_fusion.6
  98.4 0.8 convolution_add_fusion.6
  101.3 0.9 constant_dynamic-slice_fusion.6
  103.1 0.8 convolution_add_fusion.6
  105.7 1.0 add_convert_fusion.2
  (212 shorter events, 44.8 us)
Async XLA Ops:
  0.6 104.0 %copy-start = (bf16[256,128]{1,0:T(8,128)(2,1)S(1)}, bf16[256,128]{1,0:T(8,128)(2,1)}, u32[]{:S(2)}) copy-start(bf16[256,128]{1,0:T(8,128)(2,1)} %param.38) | copy-start | bytes 196612
  0.6 23.5 %copy-start.8 = (s32[1024]{0:T(1024)S(1)}, s32[1024]{0:T(1024)}, u32[]{:S(2)}) copy-start(s32[1024]{0:T(1024)} %param.26) | copy-start | bytes 12292
  2.0 22.1 %collective-permute-start.3 = (bf16[64,128]{1,0:T(8,128)(2,1)S(1)}, bf16[64,128]{1,0:T(8,128)(2,1)S(1)}, u32[]{:S(2)}, u32[]{:S(2)}) collective-permute-start(bf16[64,128]{1,0:T(8,128)(2,1)S(1)} %get-tuple-element.186), channel_id=1, source_target_pairs={{0,2},{1,3},{2,4},{3,5},{4,6},{5,7},{6,8},{7,9},{8,10},{9,11},{10,... | collective-permute-start | bytes 49160 | tf_op jit(solution)/shard_map/ppermute | solution.py:16
  7.2 16.9 %collective-permute-start.2 = (bf16[64,128]{1,0:T(8,128)(2,1)S(1)}, bf16[64,128]{1,0:T(8,128)(2,1)S(1)}, u32[]{:S(2)}, u32[]{:S(2)}) collective-permute-start(bf16[64,128]{1,0:T(8,128)(2,1)S(1)} %get-tuple-element.187), channel_id=1, source_target_pairs={{0,1},{1,2},{2,3},{3,4},{4,5},{5,6},{6,7},{7,8},{8,9},{9,10},{10,1... | collective-permute-start | bytes 49160 | tf_op jit(solution)/shard_map/ppermute | solution.py:16
  11.1 13.1 %collective-permute-start.1 = (bf16[64,128]{1,0:T(8,128)(2,1)S(1)}, bf16[64,128]{1,0:T(8,128)(2,1)S(1)}, u32[]{:S(2)}, u32[]{:S(2)}) collective-permute-start(bf16[64,128]{1,0:T(8,128)(2,1)S(1)} %get-tuple-element.188), channel_id=1, source_target_pairs={{1,0},{2,1},{3,2},{4,3},{5,4},{6,5},{7,6},{8,7},{9,8},{10,9},{11,1... | collective-permute-start | bytes 49160 | tf_op jit(solution)/shard_map/ppermute | solution.py:16
  17.3 6.8 %collective-permute-start = (bf16[64,128]{1,0:T(8,128)(2,1)S(1)}, bf16[64,128]{1,0:T(8,128)(2,1)S(1)}, u32[]{:S(2)}, u32[]{:S(2)}) collective-permute-start(bf16[64,128]{1,0:T(8,128)(2,1)S(1)} %get-tuple-element.189), channel_id=1, source_target_pairs={{2,0},{3,1},{4,2},{5,3},{6,4},{7,5},{8,6},{9,7},{10,8},{11,9},{12,... | collective-permute-start | bytes 49160 | tf_op jit(solution)/shard_map/ppermute | solution.py:16
  22.6 2.7 %copy-start.9 = (s32[1,128]{1,0:T(1,128)S(1)}, s32[1,128]{1,0:T(1,128)}, u32[]{:S(2)}) copy-start(s32[1,128]{1,0:T(1,128)} %param.27) | copy-start | bytes 1540
  24.2 9.1 %copy-start.10 = (s32[1,32]{1,0:T(1,128)S(1)}, s32[1,32]{1,0:T(1,128)}, u32[]{:S(2)}) copy-start(s32[1,32]{1,0:T(1,128)} %param.28) | copy-start | bytes 388
  24.2 22.8 %copy-start.1 = (f32[128]{0:T(128)S(1)}, f32[128]{0:T(128)}, u32[]{:S(2)}) copy-start(f32[128]{0:T(128)} %param.36) | copy-start | bytes 1540
  24.2 22.8 %copy-start.2 = (f32[128]{0:T(128)S(1)}, f32[128]{0:T(128)}, u32[]{:S(2)}) copy-start(f32[128]{0:T(128)} %param.37) | copy-start | bytes 1540
  24.2 22.8 %copy-start.5 = (bf16[384,128]{1,0:T(8,128)(2,1)S(1)}, bf16[384,128]{1,0:T(8,128)(2,1)}, u32[]{:S(2)}) copy-start(bf16[384,128]{1,0:T(8,128)(2,1)} %param.32) | copy-start | bytes 294916
  24.2 22.8 %copy-start.6 = (bf16[128,128]{1,0:T(8,128)(2,1)S(1)}, bf16[128,128]{1,0:T(8,128)(2,1)}, u32[]{:S(2)}) copy-start(bf16[128,128]{1,0:T(8,128)(2,1)} %param.34) | copy-start | bytes 98308
  24.2 22.8 %copy-start.11 = (f32[128]{0:T(128)S(1)}, f32[128]{0:T(128)}, u32[]{:S(2)}) copy-start(f32[128]{0:T(128)} %param.33) | copy-start | bytes 1540
  24.3 22.8 %copy-start.12 = (f32[128]{0:T(128)S(1)}, f32[128]{0:T(128)}, u32[]{:S(2)}) copy-start(f32[128]{0:T(128)} %param.35) | copy-start | bytes 1540
  25.6 20.0 %collective-permute-start.4 = (bf16[32,128]{1,0:T(8,128)(2,1)S(1)}, bf16[32,128]{1,0:T(8,128)(2,1)S(1)}, u32[]{:S(2)}, u32[]{:S(2)}) collective-permute-start(bf16[32,128]{1,0:T(8,128)(2,1)S(1)} %get-tuple-element.193), channel_id=1, source_target_pairs={{2,0},{3,1},{4,2},{5,3},{6,4},{7,5},{8,6},{9,7},{10,8},{11,9},{12,... | collective-permute-start | bytes 24584 | tf_op jit(solution)/shard_map/ppermute | solution.py:16
  33.5 13.5 %collective-permute-start.8 = (bf16[32,128]{1,0:T(8,128)(2,1)S(1)}, bf16[32,128]{1,0:T(8,128)(2,1)S(1)}, u32[]{:S(2)}, u32[]{:S(2)}) collective-permute-start(bf16[32,128]{1,0:T(8,128)(2,1)S(1)} %convolution_convert_fusion.2), channel_id=1, source_target_pairs={{0,128},{128,0},{1,129},{129,1},{2,130},{130,2},{3,131},{131,3},{4... | collective-permute-start | bytes 24584 | tf_op jit(solution)/shard_map/ppermute | solution.py:20
  33.6 13.4 %collective-permute-start.7 = (bf16[32,128]{1,0:T(8,128)(2,1)S(1)}, bf16[32,128]{1,0:T(8,128)(2,1)S(1)}, u32[]{:S(2)}, u32[]{:S(2)}) collective-permute-start(bf16[32,128]{1,0:T(8,128)(2,1)S(1)} %get-tuple-element.190), channel_id=1, source_target_pairs={{0,2},{1,3},{2,4},{3,5},{4,6},{5,7},{6,8},{7,9},{8,10},{9,11},{10,... | collective-permute-start | bytes 24584 | tf_op jit(solution)/shard_map/ppermute | solution.py:16
  35.5 11.4 %collective-permute-start.6 = (bf16[32,128]{1,0:T(8,128)(2,1)S(1)}, bf16[32,128]{1,0:T(8,128)(2,1)S(1)}, u32[]{:S(2)}, u32[]{:S(2)}) collective-permute-start(bf16[32,128]{1,0:T(8,128)(2,1)S(1)} %get-tuple-element.191), channel_id=1, source_target_pairs={{0,1},{1,2},{2,3},{3,4},{4,5},{5,6},{6,7},{7,8},{8,9},{9,10},{10,1... | collective-permute-start | bytes 24584 | tf_op jit(solution)/shard_map/ppermute | solution.py:16
  37.9 9.1 %collective-permute-start.5 = (bf16[32,128]{1,0:T(8,128)(2,1)S(1)}, bf16[32,128]{1,0:T(8,128)(2,1)S(1)}, u32[]{:S(2)}, u32[]{:S(2)}) collective-permute-start(bf16[32,128]{1,0:T(8,128)(2,1)S(1)} %get-tuple-element.192), channel_id=1, source_target_pairs={{1,0},{2,1},{3,2},{4,3},{5,4},{6,5},{7,6},{8,7},{9,8},{10,9},{11,1... | collective-permute-start | bytes 24584 | tf_op jit(solution)/shard_map/ppermute | solution.py:16
  47.1 57.6 %copy-start.7 = (bf16[128,128]{1,0:T(8,128)(2,1)S(1)}, bf16[128,128]{1,0:T(8,128)(2,1)}, u32[]{:S(2)}) copy-start(bf16[128,128]{1,0:T(8,128)(2,1)} %param.40) | copy-start | bytes 98308
  47.1 57.6 %copy-start.13 = (f32[128]{0:T(128)S(1)}, f32[128]{0:T(128)}, u32[]{:S(2)}) copy-start(f32[128]{0:T(128)} %param.41) | copy-start | bytes 1540
  47.1 57.6 %copy-start.14 = (f32[128]{0:T(128)S(1)}, f32[128]{0:T(128)}, u32[]{:S(2)}) copy-start(f32[128]{0:T(128)} %param.39) | copy-start | bytes 1540
  104.6 1.1 %copy-start.3 = (f32[128]{0:T(128)S(1)}, f32[128]{0:T(128)}, u32[]{:S(2)}) copy-start(f32[128]{0:T(128)} %param.43) | copy-start | bytes 1540
  104.6 1.1 %copy-start.4 = (f32[128]{0:T(128)S(1)}, f32[128]{0:T(128)}, u32[]{:S(2)}) copy-start(f32[128]{0:T(128)} %param.42) | copy-start | bytes 1540
where the time goes:
time: 108 us; the launch traced here: 107 us
  starting transfers between devices  38.5 us (36%)
  matrix products  35.5 us (33%)
  local copies, waits for them, and re-layouts  25.4 us (24%)
  other arithmetic  4.16 us (4%)
  waiting for transfers between devices  1.34 us (1%)
    ppermute x8, starting transfers between devices, passed_along(): lax.ppermute(value, axis, [(source, source + steps) for source in range(f...  38.4 us
    dynamic_slice x36, local copies, waits for them, and re-layouts, body(): lax.scan(edge_block, jnp.zeros((node_count, latent), jnp.float32), (edge_...  12.5 us
    dot_general x16, matrix products, select_rows(): jnp.dot(marks, source_rows, preferred_element_type=jnp.float32)  11.8 us
    dot_general x12, matrix products, edge_block(): lax.dot_general(marks, kept, (((0,), (0,)), ((), ())), preferred_element_...  9.63 us
    dynamic_update_slice x24, local copies, waits for them, and re-layouts, body(): lax.scan(edge_block, jnp.zeros((node_count, latent), jnp.float32), (edge_...  9.45 us
    dot_general x12, matrix products, edge_block(): jnp.dot(marks, fresh, preferred_element_type=jnp.float32)  7.65 us
    dot_general x12, matrix products, edge_block(): jnp.dot(hidden, edge_w2, preferred_element_type=jnp.float32) + edge_b2  5.76 us
  transfers between devices with their start and end apart: 9, of which 1 were waited for; matrix products, arithmetic and copies ran while one was open for 3% of the time, Pallas kernels for 0%

commit v1 on v0

v1 whole, which is shorter than its diff:
```python
import functools

import jax
import jax.numpy as jnp
from jax import lax
from jax.experimental import pallas as pl
from jax.experimental.pallas import tpu as pltpu
from jax.sharding import PartitionSpec as P

R = 2
EPSILON = 1e-05
L = 128
TILE = 512
HALF = 512
MESH = pl.DeviceIdType.MESH
F32, BF16, I32, I16 = jnp.float32, jnp.bfloat16, jnp.int32, jnp.int16


def offset_list():
    return [number - R if number < R else number - R + 1 for number in range(2 * R)]


def dot(a, b):
    return jnp.dot(a, b, preferred_element_type=F32)


def down(row):
    return jnp.broadcast_to(row, (128, 128)).T


def one_hot(column, first, width):
    small = column.astype(I16)
    lanes = lax.broadcasted_iota(I32, (column.shape[0], 128), 1).astype(I16)
    pieces = []
    for start in range(0, width, 128):
        hit = (small - jnp.int16(first + start)) == lanes
        pieces.append(jnp.where(hit, jnp.bfloat16(1), jnp.bfloat16(0)))
    return jnp.concatenate(pieces, axis=1)


def layer_norm(values, gain, bias):
    center = values - jnp.mean(values, axis=-1, keepdims=True)
    spread = jnp.mean(center * center, axis=-1, keepdims=True)
    return center * lax.rsqrt(spread + EPSILON) * gain + bias


def exchange_kernel(count, old_ref, ms_ref, mr_ref, hs_ref, xs_ref, fresh_ref, halo_ref,
                    leave_buf, arrive_buf, out_buf, in_buf,
                    lsend, lrecv, hsend, hrecv):
    me = lax.axis_index("dom")
    other = 1 - lax.axis_index("grp")
    shifts = offset_list()
    peers = [lax.rem(me + shift + count, count) for shift in shifts]

    barrier = pltpu.get_barrier_semaphore()
    for peer in peers:
        pl.semaphore_signal(barrier, inc=1, device_id={"dom": peer}, device_id_type=MESH)
    pl.semaphore_signal(barrier, inc=1, device_id={"grp": other}, device_id_type=MESH)

    old = old_ref[...]
    nodes = old.shape[0]
    moves = ms_ref.shape[1] // len(shifts)
    halos = hs_ref.shape[1] // len(shifts)
    want = jnp.concatenate([down(ms_ref[:, i:i + 128]) for i in range(0, ms_ref.shape[1], 128)], axis=0)
    leave_buf[...] = dot(one_hot(want, 0, nodes), old).astype(BF16)
    pl.semaphore_wait(barrier, len(peers) + 1)

    copies = []
    for place, peer in enumerate(peers):
        rows = pl.ds(place * moves, moves)
        copy = pltpu.make_async_remote_copy(
            src_ref=leave_buf.at[rows], dst_ref=arrive_buf.at[rows],
            send_sem=lsend.at[place], recv_sem=lrecv.at[place],
            device_id={"dom": peer}, device_id_type=MESH)
        copy.start()
        copies.append(copy)

    take = jnp.concatenate([down(mr_ref[i:i + 1, :]) for i in range(mr_ref.shape[0])], axis=0)
    stay = dot(one_hot(take, 0, nodes), old)
    new = one_hot(take, nodes, arrive_buf.shape[0])
    hwant = jnp.concatenate([down(hs_ref[...]), down(xs_ref[...])[:32]], axis=0)
    hot = one_hot(hwant, 0, nodes)
    for copy in copies:
        copy.wait_recv()
    fresh = (stay + dot(new, arrive_buf[...])).astype(BF16)
    fresh_ref[...] = fresh
    out_buf[...] = dot(hot, fresh).astype(BF16)

    second = []
    for place, peer in enumerate(peers):
        rows = pl.ds(place * halos, halos)
        copy = pltpu.make_async_remote_copy(
            src_ref=out_buf.at[rows], dst_ref=in_buf.at[rows],
            send_sem=hsend.at[place], recv_sem=hrecv.at[place],
            device_id={"dom": peer}, device_id_type=MESH)
        copy.start()
        second.append(copy)
    rows = pl.ds(len(peers) * halos, 32)
    copy = pltpu.make_async_remote_copy(
        src_ref=out_buf.at[rows], dst_ref=in_buf.at[rows],
        send_sem=hsend.at[len(peers)], recv_sem=hrecv.at[len(peers)],
        device_id={"grp": other}, device_id_type=MESH)
    copy.start()
    second.append(copy)
    for copy in copies:
        copy.wait_send()
    for copy in second:
        copy.wait()
    halo_ref[...] = in_buf[...]


def layer_kernel(fresh_ref, halo_ref, snd_ref, rcv_ref, live_ref,
                 ew1_ref, eb1_ref, ew2_ref, eb2_ref, eg_ref, eo_ref,
                 nw1_ref, nb1_ref, nw2_ref, nb2_ref, ng_ref, no_ref, edge_hbm,
                 node_out, edge_out,
                 edge_buf, new_buf, send_tab, recv_tab, words, pre_buf, sums, in_sem, out_sem):
    edges = edge_buf.shape[0]
    tiles = edges // TILE
    subs = TILE // 128
    loads = [pltpu.make_async_copy(edge_hbm.at[pl.ds(i * TILE, TILE)], edge_buf.at[pl.ds(i * TILE, TILE)], in_sem.at[i])
             for i in range(tiles)]
    for load in loads:
        load.start()

    fresh = fresh_ref[...]
    halo = halo_ref[...]
    w1e, w1s, w1r = ew1_ref[0:L], ew1_ref[L:2 * L], ew1_ref[2 * L:3 * L]
    part = dot(fresh, w1s).astype(BF16)
    far = dot(halo, w1s).astype(BF16)
    send_tab[0:HALF, 0:L] = part[:HALF]
    send_tab[0:HALF, L:2 * L] = part[HALF:]
    send_tab[HALF:HALF + 128, 0:L] = far[:128]
    send_tab[HALF:HALF + 32, L:2 * L] = far[128:]
    send_tab[HALF + 32:HALF + 128, L:2 * L] = jnp.zeros((96, L), BF16)
    send_tab[HALF + 128:, 0:L] = w1e
    send_tab[HALF + 128:, L:2 * L] = w1e
    part = dot(fresh, w1r).astype(BF16)
    recv_tab[:, 0:L] = part[:HALF]
    recv_tab[:, L:2 * L] = part[HALF:]

    s, r, live = snd_ref[...], rcv_ref[...], live_ref[...]
    far_s = s >= 2 * HALF
    q = s - 2 * HALF
    s_row = jnp.where(far_s, HALF + (q & 127), s & (HALF - 1))
    s_half = jnp.where(far_s, q >> 7, s >> 9)
    r_row = r & (HALF - 1)
    r_half = r >> 9
    words[...] = s_row | (s_half << 10) | (r_row << 11) | (r_half << 21) | (live << 22)
    sums[...] = jnp.zeros_like(sums)

    w2 = ew2_ref[...]
    nil = jnp.zeros((L, L), BF16)
    w2_pair = jnp.concatenate([jnp.concatenate([w2, nil], axis=1), jnp.concatenate([nil, w2], axis=1)], axis=0)

    for tile in range(tiles):
        loads[tile].wait()
        spot = pl.ds(tile * TILE, TILE)
        word = jnp.concatenate([down(words[tile * subs + i:tile * subs + i + 1, :]) for i in range(subs)], axis=0)
        edge = edge_buf[spot]
        hot_s = jnp.concatenate([one_hot(word & 1023, 0, HALF + 128), edge], axis=1)
        got_s = dot(hot_s, send_tab[...])
        got_r = dot(one_hot((word >> 11) & 1023, 0, HALF), recv_tab[...])
        pre = (jnp.where((word & (1 << 10)) != 0, got_s[:, L:], got_s[:, :L])
               + jnp.where((word & (1 << 21)) != 0, got_r[:, L:], got_r[:, :L]))
        hidden = jnp.maximum(pre + eb1_ref[...], 0.0).astype(BF16)
        pair = jnp.concatenate([hidden[:TILE // 2], hidden[TILE // 2:]], axis=1)
        before = dot(pair, w2_pair)
        before = jnp.concatenate([before[:, :L], before[:, L:]], axis=0) + eb2_ref[...]
        message = layer_norm(before, eg_ref[...], eo_ref[...])
        kept = jnp.where((word & (1 << 22)) != 0, message, 0.0).astype(BF16)
        new_buf[spot] = (edge.astype(F32) + kept.astype(F32)).astype(BF16)
        pltpu.make_async_copy(new_buf.at[spot], edge_out.at[spot], out_sem.at[tile]).start()
        upper = ((word >> 11) & 1024).astype(I16) != jnp.int16(0)
        zero = jnp.zeros_like(kept)
        sides = jnp.concatenate([jnp.where(upper, zero, kept), jnp.where(upper, kept, zero)], axis=1)
        down_iota = lax.broadcasted_iota(I32, (HALF, 128), 0).astype(I16)
        flat = []
        for i in range(subs):
            row = (words[tile * subs + i:tile * subs + i + 1, :] >> 11) & 1023
            flat.append(jnp.where(jnp.broadcast_to(row, (HALF, 128)).astype(I16) == down_iota,
                                  jnp.bfloat16(1), jnp.bfloat16(0)))
        sums[...] += dot(jnp.concatenate(flat, axis=1), sides)

    inbound = jnp.concatenate([sums[:, :L], sums[:, L:]], axis=0).astype(BF16)
    node_in = jnp.concatenate([fresh, inbound], axis=1)
    node_hidden = jnp.maximum(dot(node_in, nw1_ref[...]) + nb1_ref[...], 0.0).astype(BF16)
    before = dot(node_hidden, nw2_ref[...]) + nb2_ref[...]
    node_out[...] = (fresh.astype(F32) + layer_norm(before, ng_ref[...], no_ref[...])).astype(BF16)
    for tile in range(tiles):
        spot = pl.ds(tile * TILE, TILE)
        pltpu.make_async_copy(new_buf.at[spot], edge_out.at[spot], out_sem.at[tile]).wait()


VM = pl.BlockSpec(memory_space=pltpu.VMEM)
ANY = pl.BlockSpec(memory_space=pl.ANY)


def exchange(count, old, mig_send, mig_recv, halo_send, cross_send):
    nodes = old.shape[0]
    far = halo_send.shape[1] + cross_send.shape[1]
    steps = 2 * R
    padded = jnp.pad(cross_send, ((0, 0), (0, 128 - cross_send.shape[1])), constant_values=nodes)
    return pl.pallas_call(
        functools.partial(exchange_kernel, count),
        out_shape=(jax.ShapeDtypeStruct((nodes, L), BF16), jax.ShapeDtypeStruct((far, L), BF16)),
        in_specs=[VM] * 5,
        out_specs=(VM, VM),
        scratch_shapes=[
            pltpu.VMEM((mig_send.shape[1], L), BF16),
            pltpu.VMEM((mig_send.shape[1], L), BF16),
            pltpu.VMEM((far, L), BF16),
            pltpu.VMEM((far, L), BF16),
            pltpu.SemaphoreType.DMA((steps,)),
            pltpu.SemaphoreType.DMA((steps,)),
            pltpu.SemaphoreType.DMA((steps + 1,)),
            pltpu.SemaphoreType.DMA((steps + 1,)),
        ],
        compiler_params=pltpu.CompilerParams(collective_id=0, has_side_effects=True, vmem_limit_bytes=16 << 20),
        name="exchange",
    )(old, mig_send, mig_recv.reshape(-1, 128), halo_send, padded)


def layer(fresh, halo, edge_latent, senders, receivers, edge_live, weights):
    nodes, edges = fresh.shape[0], edge_latent.shape[0]
    vectors = [w if w.ndim == 2 else w.reshape(1, -1) for w in weights]
    lines = [v.reshape(-1, 128) for v in (senders, receivers, edge_live)]
    return pl.pallas_call(
        layer_kernel,
        out_shape=(jax.ShapeDtypeStruct((nodes, L), BF16), jax.ShapeDtypeStruct((edges, L), BF16)),
        in_specs=[VM] * (5 + len(vectors)) + [ANY],
        out_specs=(VM, ANY),
        scratch_shapes=[
            pltpu.VMEM((edges, L), BF16),
            pltpu.VMEM((edges, L), BF16),
            pltpu.VMEM((HALF + 256, 2 * L), BF16),
            pltpu.VMEM((HALF, 2 * L), BF16),
            pltpu.VMEM((edges // 128, 128), I32),
            pltpu.VMEM((2, TILE, L), F32),
            pltpu.VMEM((HALF, 2 * L), F32),
            pltpu.SemaphoreType.DMA((edges // TILE,)),
            pltpu.SemaphoreType.DMA((edges // TILE,)),
        ],
        compiler_params=pltpu.CompilerParams(vmem_limit_bytes=40 << 20),
        name="layer",
    )(fresh, halo, *lines, *vectors, edge_latent)


def solution(mesh):
    count = mesh.shape["dom"]

    def body(node_latent, edge_latent, mig_send, mig_recv, halo_send, cross_send, senders, receivers, edge_live,
             *weights):
        fresh, halo = exchange(count, node_latent, mig_send, mig_recv, halo_send, cross_send)
        return layer(fresh, halo, edge_latent, senders, receivers, edge_live, weights)

    rows, line = P(("grp", "dom"), None), P(("grp", "dom"))
    return jax.shard_map(
        body,
        mesh=mesh,
        in_specs=(rows, rows, rows, line, rows, rows, line, line, line) + (P(),) * 12,
        out_specs=(rows, rows),
        check_vma=False,
    )
```

time: 108 us -> 59.3 us (0.55)
  the two profiles are of different devices: /device:TPU:24 before, /device:TPU:32 now
where the time goes in v1:
time: 59.3 us; the launch traced here: 58.6 us
  Pallas kernels  42.3 us (71%)
  local copies, waits for them, and re-layouts  15.7 us (26%)
  between operations  0.67 us (1%)
    pallas_call x1, Pallas kernels, exchange(): pl.pallas_call(functools.partial(exchange_kernel, count), out_shape=(jax....  23.2 us
    pallas_call x1, Pallas kernels, layer(): pl.pallas_call(layer_kernel, out_shape=(jax.ShapeDtypeStruct((nodes, L),...  19.1 us
    unnamed x40, local copies, waits for them, and re-layouts  15.1 us

profile of v1, /device:TPU:32, one launch (start us, length us, event | category | flops | bytes accessed | tf_op | source)
XLA Modules:
  0.0 58.6 jit_solution(8888699174416398703)
XLA Ops:
  0.6 0.7 %pad.4.xs_ref = s32[1,128]{1,0:T(1,128)S(1)} pad(s32[1,32]{1,0:T(1,128)} %param.26, s32[]{:T(128)} %constant.0.clone.1), padding=0_0x0_96 | pad | bytes 644 | tf_op jit(solution)/shard_map/jit(_pad)/pad | solution.py:202
  1.3 0.0 copy-start.1
  1.3 0.9 %copy-done.1 = bf16[1024,128]{1,0:T(8,128)(2,1)S(1)} copy-done((bf16[1024,128]{1,0:T(8,128)(2,1)S(1)}, bf16[1024,128]{1,0:T(8,128)(2,1)}, u32[]{:S(2)}) %copy-start.1) | copy-done | bytes 262168
  2.2 0.0 copy-start.9
  2.2 0.7 %copy-done.9 = s32[1024]{0:T(1024)S(1)} copy-done((s32[1024]{0:T(1024)S(1)}, s32[1024]{0:T(1024)}, u32[]{:S(2)}) %copy-start.9) | copy-done | bytes 4120
  2.9 0.0 copy-start.10
  2.9 0.7 %copy-done.10 = s32[1,256]{1,0:T(1,128)S(1)} copy-done((s32[1,256]{1,0:T(1,128)S(1)}, s32[1,256]{1,0:T(1,128)}, u32[]{:S(2)}) %copy-start.10) | copy-done | bytes 1048
  3.6 0.0 copy-start.11
  3.6 0.7 %copy-done.11 = s32[1,128]{1,0:T(1,128)S(1)} copy-done((s32[1,128]{1,0:T(1,128)S(1)}, s32[1,128]{1,0:T(1,128)}, u32[]{:S(2)}) %copy-start.11) | copy-done | bytes 536
  4.3 23.2 %exchange.1 = (bf16[1024,128]{1,0:T(8,128)(2,1)S(1)}, bf16[160,128]{1,0:T(8,128)(2,1)S(1)}) custom-call(bf16[1024,128]{1,0:T(8,128)(2,1)S(1)} %copy-done.1, s32[1,256]{1,0:T(1,128)S(1)} %copy-done.10, s32[8,128]{1,0:T(8,128)S(1)} %bitcast.15, s32[1,128]{1,0:T(1,128)S(1)} %copy-done.11, s32[1,128]{1,0:T(1,128)S(1)} %pad.4.xs_ref), custom_call_target="tpu_custom_call" | custom-call | tf_op jit(solution)/shard_map/exchange/pallas_call | solution.py:203
  27.4 0.0 copy-start
  27.4 1.4 %copy-done = bf16[6144,128]{1,0:T(8,128)(2,1)S(1)} copy-done((bf16[6144,128]{1,0:T(8,128)(2,1)S(1)}, bf16[6144,128]{1,0:T(8,128)(2,1)}, u32[]{:S(2)}) %copy-start) | copy-done | bytes 1572888
  28.8 0.0 copy-start.2
  28.8 0.9 %copy-done.2 = bf16[384,128]{1,0:T(8,128)(2,1)S(1)} copy-done((bf16[384,128]{1,0:T(8,128)(2,1)S(1)}, bf16[384,128]{1,0:T(8,128)(2,1)}, u32[]{:S(2)}) %copy-start.2) | copy-done | bytes 98328
  29.7 0.0 copy-start.3
  29.7 0.8 %copy-done.3 = bf16[256,128]{1,0:T(8,128)(2,1)S(1)} copy-done((bf16[256,128]{1,0:T(8,128)(2,1)S(1)}, bf16[256,128]{1,0:T(8,128)(2,1)}, u32[]{:S(2)}) %copy-start.3) | copy-done | bytes 65560
  30.6 0.0 copy-start.4
  30.6 0.8 %copy-done.4 = bf16[128,128]{1,0:T(8,128)(2,1)S(1)} copy-done((bf16[128,128]{1,0:T(8,128)(2,1)S(1)}, bf16[128,128]{1,0:T(8,128)(2,1)}, u32[]{:S(2)}) %copy-start.4) | copy-done | bytes 32792
  31.3 0.0 copy-start.5
  31.3 0.8 %copy-done.5 = bf16[128,128]{1,0:T(8,128)(2,1)S(1)} copy-done((bf16[128,128]{1,0:T(8,128)(2,1)S(1)}, bf16[128,128]{1,0:T(8,128)(2,1)}, u32[]{:S(2)}) %copy-start.5) | copy-done | bytes 32792
  32.1 0.7 %copy-done.6 = s32[6144]{0:T(1024)S(1)} copy-done((s32[6144]{0:T(1024)S(1)}, s32[6144]{0:T(1024)}, u32[]{:S(2)}) %copy-start.6) | copy-done | bytes 24600
  32.8 0.7 %copy-done.7 = s32[6144]{0:T(1024)S(1)} copy-done((s32[6144]{0:T(1024)S(1)}, s32[6144]{0:T(1024)}, u32[]{:S(2)}) %copy-start.7) | copy-done | bytes 24600
  33.6 0.7 %copy-done.8 = s32[6144]{0:T(1024)S(1)} copy-done((s32[6144]{0:T(1024)S(1)}, s32[6144]{0:T(1024)}, u32[]{:S(2)}) %copy-start.8) | copy-done | bytes 24600
  34.3 0.7 %copy-done.12 = f32[128]{0:T(128)S(1)} copy-done((f32[128]{0:T(128)S(1)}, f32[128]{0:T(128)}, u32[]{:S(2)}) %copy-start.12) | copy-done | bytes 536
  35.0 0.7 %copy-done.13 = f32[128]{0:T(128)S(1)} copy-done((f32[128]{0:T(128)S(1)}, f32[128]{0:T(128)}, u32[]{:S(2)}) %copy-start.13) | copy-done | bytes 536
  35.6 0.7 %copy-done.14 = f32[128]{0:T(128)S(1)} copy-done((f32[128]{0:T(128)S(1)}, f32[128]{0:T(128)}, u32[]{:S(2)}) %copy-start.14) | copy-done | bytes 536
  36.3 0.7 %copy-done.15 = f32[128]{0:T(128)S(1)} copy-done((f32[128]{0:T(128)S(1)}, f32[128]{0:T(128)}, u32[]{:S(2)}) %copy-start.15) | copy-done | bytes 536
  36.9 0.7 %copy-done.16 = f32[128]{0:T(128)S(1)} copy-done((f32[128]{0:T(128)S(1)}, f32[128]{0:T(128)}, u32[]{:S(2)}) %copy-start.16) | copy-done | bytes 536
  37.6 0.7 %copy-done.17 = f32[128]{0:T(128)S(1)} copy-done((f32[128]{0:T(128)S(1)}, f32[128]{0:T(128)}, u32[]{:S(2)}) %copy-start.17) | copy-done | bytes 536
  38.2 0.7 %copy-done.18 = f32[128]{0:T(128)S(1)} copy-done((f32[128]{0:T(128)S(1)}, f32[128]{0:T(128)}, u32[]{:S(2)}) %copy-start.18) | copy-done | bytes 536
  38.9 0.7 %copy-done.19 = f32[128]{0:T(128)S(1)} copy-done((f32[128]{0:T(128)S(1)}, f32[128]{0:T(128)}, u32[]{:S(2)}) %copy-start.19) | copy-done | bytes 536
  39.6 19.1 %layer.1 = (bf16[1024,128]{1,0:T(8,128)(2,1)}, bf16[6144,128]{1,0:T(8,128)(2,1)}) custom-call(bf16[1024,128]{1,0:T(8,128)(2,1)S(1)} %get-tuple-element.4.fresh_ref, bf16[160,128]{1,0:T(8,128)(2,1)S(1)} %get-tuple-element.5.halo_ref, s32[48,128]{1,0:T(8,128)S(1)} %bitcast.12, s32[48,128]{1,0:T(8,128)S(1)} %bitcast.13, s32[48,128]{1,0:T(8,128)S(1)} %bitcast.14, ...), custom_call_target="tpu_custom_call" | custom-call | tf_op jit(solution)/shard_map/layer/pallas_call | solution.py:227
  (11 shorter events, 0.0 us)
Async XLA Ops:
  1.3 0.9 %copy-start.1 = (bf16[1024,128]{1,0:T(8,128)(2,1)S(1)}, bf16[1024,128]{1,0:T(8,128)(2,1)}, u32[]{:S(2)}) copy-start(bf16[1024,128]{1,0:T(8,128)(2,1)} %old_ref.1) | copy-start | bytes 786436
  2.2 0.7 %copy-start.9 = (s32[1024]{0:T(1024)S(1)}, s32[1024]{0:T(1024)}, u32[]{:S(2)}) copy-start(s32[1024]{0:T(1024)} %param.24) | copy-start | bytes 12292
  2.9 0.7 %copy-start.10 = (s32[1,256]{1,0:T(1,128)S(1)}, s32[1,256]{1,0:T(1,128)}, u32[]{:S(2)}) copy-start(s32[1,256]{1,0:T(1,128)} %ms_ref.1) | copy-start | bytes 3076
  3.6 0.7 %copy-start.11 = (s32[1,128]{1,0:T(1,128)S(1)}, s32[1,128]{1,0:T(1,128)}, u32[]{:S(2)}) copy-start(s32[1,128]{1,0:T(1,128)} %hs_ref.1) | copy-start | bytes 1540
  27.4 1.4 %copy-start = (bf16[6144,128]{1,0:T(8,128)(2,1)S(1)}, bf16[6144,128]{1,0:T(8,128)(2,1)}, u32[]{:S(2)}) copy-start(bf16[6144,128]{1,0:T(8,128)(2,1)} %edge_hbm.1) | copy-start | bytes 4718596
  28.8 0.9 %copy-start.2 = (bf16[384,128]{1,0:T(8,128)(2,1)S(1)}, bf16[384,128]{1,0:T(8,128)(2,1)}, u32[]{:S(2)}) copy-start(bf16[384,128]{1,0:T(8,128)(2,1)} %ew1_ref.1) | copy-start | bytes 294916
  29.7 0.8 %copy-start.3 = (bf16[256,128]{1,0:T(8,128)(2,1)S(1)}, bf16[256,128]{1,0:T(8,128)(2,1)}, u32[]{:S(2)}) copy-start(bf16[256,128]{1,0:T(8,128)(2,1)} %nw1_ref.1) | copy-start | bytes 196612
  30.6 0.8 %copy-start.4 = (bf16[128,128]{1,0:T(8,128)(2,1)S(1)}, bf16[128,128]{1,0:T(8,128)(2,1)}, u32[]{:S(2)}) copy-start(bf16[128,128]{1,0:T(8,128)(2,1)} %ew2_ref.1) | copy-start | bytes 98308
  31.3 0.8 %copy-start.5 = (bf16[128,128]{1,0:T(8,128)(2,1)S(1)}, bf16[128,128]{1,0:T(8,128)(2,1)}, u32[]{:S(2)}) copy-start(bf16[128,128]{1,0:T(8,128)(2,1)} %nw2_ref.1) | copy-start | bytes 98308
  32.1 0.7 %copy-start.6 = (s32[6144]{0:T(1024)S(1)}, s32[6144]{0:T(1024)}, u32[]{:S(2)}) copy-start(s32[6144]{0:T(1024)} %param.27) | copy-start | bytes 73732
  32.8 0.7 %copy-start.7 = (s32[6144]{0:T(1024)S(1)}, s32[6144]{0:T(1024)}, u32[]{:S(2)}) copy-start(s32[6144]{0:T(1024)} %param.28) | copy-start | bytes 73732
  33.6 0.7 %copy-start.8 = (s32[6144]{0:T(1024)S(1)}, s32[6144]{0:T(1024)}, u32[]{:S(2)}) copy-start(s32[6144]{0:T(1024)} %param.29) | copy-start | bytes 73732
  34.3 0.7 %copy-start.12 = (f32[128]{0:T(128)S(1)}, f32[128]{0:T(128)}, u32[]{:S(2)}) copy-start(f32[128]{0:T(128)} %param.31) | copy-start | bytes 1540
  35.0 0.7 %copy-start.13 = (f32[128]{0:T(128)S(1)}, f32[128]{0:T(128)}, u32[]{:S(2)}) copy-start(f32[128]{0:T(128)} %param.33) | copy-start | bytes 1540
  35.6 0.7 %copy-start.14 = (f32[128]{0:T(128)S(1)}, f32[128]{0:T(128)}, u32[]{:S(2)}) copy-start(f32[128]{0:T(128)} %param.34) | copy-start | bytes 1540
  36.3 0.7 %copy-start.15 = (f32[128]{0:T(128)S(1)}, f32[128]{0:T(128)}, u32[]{:S(2)}) copy-start(f32[128]{0:T(128)} %param.35) | copy-start | bytes 1540
  36.9 0.7 %copy-start.16 = (f32[128]{0:T(128)S(1)}, f32[128]{0:T(128)}, u32[]{:S(2)}) copy-start(f32[128]{0:T(128)} %param.37) | copy-start | bytes 1540
  37.6 0.7 %copy-start.17 = (f32[128]{0:T(128)S(1)}, f32[128]{0:T(128)}, u32[]{:S(2)}) copy-start(f32[128]{0:T(128)} %param.39) | copy-start | bytes 1540
  38.2 0.7 %copy-start.18 = (f32[128]{0:T(128)S(1)}, f32[128]{0:T(128)}, u32[]{:S(2)}) copy-start(f32[128]{0:T(128)} %param.40) | copy-start | bytes 1540
  38.9 0.7 %copy-start.19 = (f32[128]{0:T(128)S(1)}, f32[128]{0:T(128)}, u32[]{:S(2)}) copy-start(f32[128]{0:T(128)} %param.41) | copy-start | bytes 1540

commit v2 on v1

v2 whole, which is shorter than its diff:
```python
import functools

import jax
import jax.numpy as jnp
from jax import lax
from jax.experimental import pallas as pl
from jax.experimental.pallas import tpu as pltpu
from jax.sharding import PartitionSpec as P

R = 2
EPSILON = 1e-05
L = 128
HALF = 512
WORD_TILE = 512
GATHER_TILE = 1024
TILE = 1024
MESH = pl.DeviceIdType.MESH
F32, BF16, I32, I16 = jnp.float32, jnp.bfloat16, jnp.int32, jnp.int16
UPPER_S, UPPER_R, LIVE = 30, 29, 28


def offset_list():
    return [number - R if number < R else number - R + 1 for number in range(2 * R)]


def dot(a, b):
    return jnp.dot(a, b, preferred_element_type=F32)


def down(row):
    return jnp.broadcast_to(row, (128, 128)).T


def lanes_from(first):
    return (lax.broadcasted_iota(I32, (16, 128), 1) + first).astype(I16)


def one_hot(column, first, width):
    pieces = []
    for start in range(0, width, 128):
        lanes = jnp.concatenate([lanes_from(first + start)] * (column.shape[0] // 16), axis=0)
        pieces.append(jnp.where(column == lanes, jnp.bfloat16(1), jnp.bfloat16(0)))
    return jnp.concatenate(pieces, axis=1) if len(pieces) > 1 else pieces[0]


def layer_norm(values, gain, bias):
    center = values - jnp.mean(values, axis=-1, keepdims=True)
    spread = jnp.mean(center * center, axis=-1, keepdims=True)
    return center * lax.rsqrt(spread + EPSILON) * gain + bias


def spot_of(step, size):
    return pl.ds(pl.multiple_of(step * size, size), size)


def exchange_kernel(count, old_hbm, ms_hbm, mr_hbm, hs_hbm, xs_hbm, snd_hbm, rcv_hbm, live_hbm, edge_hbm, *rest):
    weights_hbm, rest = rest[:12], rest[12:]
    fresh_ref, far_ref, pre_ref, words_ref, send_ref, rows_ref, edge_ref = rest[:7]
    weights = rest[7:19]
    (old_ref, ms_ref, mr_ref, hs_ref, xs_ref, snd_ref, rcv_ref, live_ref, recv_ref, send_tab, recv_tab,
     leave_buf, arrive_buf, out_buf, in_buf, in_sem, w_sem, lsend, lrecv, hsend, hrecv) = rest[19:]
    shifts = offset_list()
    steps = len(shifts)
    loads = [pltpu.make_async_copy(src, dst, in_sem.at[i]) for i, (src, dst) in enumerate([
        (ms_hbm, ms_ref), (old_hbm, old_ref), (mr_hbm, mr_ref), (hs_hbm, hs_ref), (xs_hbm, xs_ref),
        (snd_hbm, snd_ref), (rcv_hbm, rcv_ref), (live_hbm, live_ref), (edge_hbm, edge_ref)])]
    loads += [pltpu.make_async_copy(src, dst, w_sem.at[i]) for i, (src, dst) in enumerate(zip(weights_hbm, weights))]

    arrive_buf[...] = jnp.zeros_like(arrive_buf)
    in_buf[...] = jnp.zeros_like(in_buf)
    if count:
        me = lax.axis_index("dom")
        other = 1 - lax.axis_index("grp")
        there = [(me + shift >= 0) & (me + shift < count) for shift in shifts]
        peers = [jnp.clip(me + shift, 0, count - 1) for shift in shifts]
        barrier = pltpu.get_barrier_semaphore()
        for peer, real in zip(peers, there):
            @pl.when(real)
            def _():
                pl.semaphore_signal(barrier, inc=1, device_id={"dom": peer}, device_id_type=MESH)
        pl.semaphore_signal(barrier, inc=1, device_id={"grp": other}, device_id_type=MESH)

    for load in loads:
        load.start()
    nodes = old_ref.shape[0]
    moves = ms_ref.shape[1] // steps
    halos = hs_ref.shape[1] // steps
    across = xs_ref.shape[1]
    loads[0].wait()
    want = jnp.concatenate([down(ms_ref[:, i:i + 128]) for i in range(0, ms_ref.shape[1], 128)], axis=0).astype(I16)
    hot = one_hot(want, 0, nodes)
    loads[1].wait()
    old = old_ref[...]
    leave_buf[...] = dot(hot, old).astype(BF16)

    def sends(src, dst, size, send_sem, recv_sem):
        made = []
        for place in range(steps):
            rows = pl.ds(place * size, size)
            made.append(pltpu.make_async_remote_copy(
                src_ref=src.at[rows], dst_ref=dst.at[rows], send_sem=send_sem.at[place], recv_sem=recv_sem.at[place],
                device_id={"dom": peers[place]}, device_id_type=MESH))
        return made

    if count:
        from_there = [there[steps - 1 - place] for place in range(steps)]
        pl.semaphore_wait(barrier, sum(real.astype(I32) for real in there) + 1)
        first = sends(leave_buf, arrive_buf, moves, lsend, lrecv)
        for copy, real in zip(first, there):
            pl.when(real)(copy.start)

    for load in loads[2:8]:
        load.wait()
    take = jnp.concatenate([down(mr_ref[i:i + 1, :]) for i in range(mr_ref.shape[0])], axis=0).astype(I16)
    stay_hot = one_hot(take, 0, nodes)
    new_hot = one_hot(take, nodes, arrive_buf.shape[0])
    hwant = jnp.concatenate([down(hs_ref[...]),
                             down(jnp.concatenate([xs_ref[...]] * (128 // across), axis=1))[:across]],
                            axis=0).astype(I16)
    halo_hot = one_hot(hwant, 0, nodes)
    via_new = dot(halo_hot, new_hot).astype(BF16)
    stay = dot(stay_hot, old)
    halo_stay = dot(halo_hot, stay.astype(BF16))

    s, r, live = snd_ref[...], rcv_ref[...], live_ref[...]
    far_s = s >= 2 * HALF
    s_row = jnp.where(far_s, s - HALF, s & (HALF - 1))
    s_up = jnp.where(far_s, 0, s >> 9)
    r_row = r & (HALF - 1)
    rows_ref[...] = r_row
    snd_ref[...] = (s_row << 16) | r_row | (s_up << UPPER_S) | ((r >> 9) << UPPER_R) | (live << LIVE)
    for load in loads[8:]:
        load.wait()
    w1e, w1s, w1r = weights[0][0:L], weights[0][L:2 * L], weights[0][2 * L:3 * L]
    edges = edge_ref.shape[0]
    subs = WORD_TILE // 128

    @pl.loop(0, edges // WORD_TILE)
    def _(step):
        spot = spot_of(step, WORD_TILE)
        word = jnp.concatenate([down(snd_ref[pl.ds(step * subs + i, 1), :]) for i in range(subs)], axis=0)
        words_ref[spot] = word
        send_ref[spot] = ((word >> 16) & 1023).astype(I16)
        recv_ref[spot] = (word & 511).astype(I16)
        pre_ref[spot] = dot(edge_ref[spot], w1e) + weights[1][...]

    if count:
        for copy, real in zip(first, from_there):
            pl.when(real)(copy.wait_recv)
    else:
        arrive_buf[...] = leave_buf[...]
    new = arrive_buf[...]
    out_buf[...] = (halo_stay + dot(via_new, new)).astype(BF16)
    if count:
        second = sends(out_buf, in_buf, halos, hsend, hrecv)
        rows = pl.ds(steps * halos, across)
        swap = pltpu.make_async_remote_copy(
            src_ref=out_buf.at[rows], dst_ref=in_buf.at[rows],
            send_sem=hsend.at[steps], recv_sem=hrecv.at[steps],
            device_id={"grp": other}, device_id_type=MESH)
        for copy, real in zip(second, there):
            pl.when(real)(copy.start)
        swap.start()

    fresh = (stay + dot(new_hot, new)).astype(BF16)
    fresh_ref[...] = fresh
    part = dot(fresh, w1s).astype(BF16)
    send_tab[:, 0:L] = part[:HALF]
    send_tab[:, L:2 * L] = part[HALF:]
    part = dot(fresh, w1r).astype(BF16)
    recv_tab[:, 0:L] = part[:HALF]
    recv_tab[:, L:2 * L] = part[HALF:]

    @pl.loop(0, edges // GATHER_TILE)
    def _(step):
        spot = spot_of(step, GATHER_TILE)
        got_s = dot(one_hot(send_ref[spot], 0, HALF), send_tab[...])
        got_r = dot(one_hot(recv_ref[spot], 0, HALF), recv_tab[...])
        word = words_ref[spot]
        pre_ref[spot] = (pre_ref[spot] + jnp.where((word & (1 << UPPER_S)) != 0, got_s[:, L:], got_s[:, :L])
                         + jnp.where((word & (1 << UPPER_R)) != 0, got_r[:, L:], got_r[:, :L]))

    if count:
        for copy, real in zip(first, there):
            pl.when(real)(copy.wait_send)
        for copy, real in zip(second, there):
            pl.when(real)(copy.wait_send)
        for copy, real in zip(second, from_there):
            pl.when(real)(copy.wait_recv)
        swap.wait()
    else:
        in_buf[...] = out_buf[...]
    far = dot(in_buf[...], w1s).astype(BF16)
    far_ref[...] = jnp.concatenate([far, jnp.zeros((far_ref.shape[0] - far.shape[0], L), BF16)], axis=0)


def layer_kernel(fresh_ref, far_ref, pre_ref, words_ref, send_ref, rows_ref, edge_ref,
                 ew1_ref, eb1_ref, ew2_ref, eb2_ref, eg_ref, eo_ref,
                 nw1_ref, nb1_ref, nw2_ref, nb2_ref, ng_ref, no_ref,
                 node_out, edge_out, new_buf, side_0, side_1, sums, out_sem):
    edges = edge_ref.shape[0]
    tiles = edges // TILE
    subs = TILE // 128
    w2 = ew2_ref[...]
    nil = jnp.zeros((L, L), BF16)
    w2_pair = jnp.concatenate([jnp.concatenate([w2, nil], axis=1), jnp.concatenate([nil, w2], axis=1)], axis=0)
    sums[...] = jnp.zeros_like(sums)

    def messages(tile, side):
        spot = spot_of(tile, TILE)
        pre = pre_ref[spot] + dot(one_hot(send_ref[spot], HALF, 256), far_ref[...])
        hidden = jnp.maximum(pre, 0.0).astype(BF16)
        pair = jnp.concatenate([hidden[:TILE // 2], hidden[TILE // 2:]], axis=1)
        before = dot(pair, w2_pair)
        before = jnp.concatenate([before[:, :L], before[:, L:]], axis=0) + eb2_ref[...]
        message = layer_norm(before, eg_ref[...], eo_ref[...])
        word = words_ref[spot]
        kept = jnp.where((word & (1 << LIVE)) != 0, message, 0.0).astype(BF16)
        new_buf[spot] = (edge_ref[spot].astype(F32) + kept.astype(F32)).astype(BF16)
        upper = ((word >> 16) & (1 << (UPPER_R - 16))).astype(I16) != jnp.int16(0)
        zero = jnp.zeros_like(kept)
        side[:, 0:L] = jnp.where(upper, zero, kept)
        side[:, L:2 * L] = jnp.where(upper, kept, zero)

    def save(tile):
        spot = spot_of(tile, TILE)
        return pltpu.make_async_copy(new_buf.at[spot], edge_out.at[spot], out_sem.at[tile])

    def gather_in(tile, side):
        below = lax.broadcasted_iota(I32, (HALF, 128), 0).astype(I16)
        flat = []
        for i in range(subs):
            row = jnp.broadcast_to(rows_ref[pl.ds(tile * subs + i, 1), :], (16, 128)).astype(I16)
            row = jnp.concatenate([row] * (HALF // 16), axis=0)
            flat.append(jnp.where(row == below, jnp.bfloat16(1), jnp.bfloat16(0)))
        sums[...] += dot(jnp.concatenate(flat, axis=1), side[...])

    messages(0, side_0)

    @pl.loop(0, tiles // 2 - 1)
    def _(step):
        tile = 2 * step
        save(tile).start()
        gather_in(tile, side_0)
        messages(tile + 1, side_1)
        save(tile + 1).start()
        gather_in(tile + 1, side_1)
        messages(tile + 2, side_0)

    save(tiles - 2).start()
    gather_in(tiles - 2, side_0)
    messages(tiles - 1, side_1)
    save(tiles - 1).start()
    gather_in(tiles - 1, side_1)

    fresh = fresh_ref[...]
    inbound = jnp.concatenate([sums[:, :L], sums[:, L:]], axis=0).astype(BF16)
    node_hidden = jnp.maximum(dot(jnp.concatenate([fresh, inbound], axis=1), nw1_ref[...]) + nb1_ref[...], 0.0).astype(BF16)
    before = dot(node_hidden, nw2_ref[...]) + nb2_ref[...]
    node_out[...] = (fresh.astype(F32) + layer_norm(before, ng_ref[...], no_ref[...])).astype(BF16)
    for tile in range(tiles):
        save(tile).wait()


VM = pl.BlockSpec(memory_space=pltpu.VMEM)
ANY = pl.BlockSpec(memory_space=pl.ANY)
HBM = pl.BlockSpec(memory_space=pltpu.HBM)


def in_hbm(x):
    return pltpu.with_memory_space_constraint(x, pltpu.HBM)


def exchange(count, old, mig_send, mig_recv, halo_send, cross_send, lines, edge_latent, vectors):
    nodes, edges = old.shape[0], edge_latent.shape[0]
    far = halo_send.shape[1] + cross_send.shape[1]
    steps = 2 * R
    kept = [((nodes, L), BF16), ((256, L), BF16), ((edges, L), F32), ((edges, L), I32), ((edges, L), I16),
            (lines[0].shape, I32), ((edges, L), BF16)] + [(v.shape, v.dtype) for v in vectors]
    operands = [old, mig_send, mig_recv.reshape(-1, 128), halo_send, cross_send, *lines, edge_latent, *vectors]
    params = dict(collective_id=0) if count else {}
    return pl.pallas_call(
        functools.partial(exchange_kernel, count),
        out_shape=tuple(pltpu.VMEM(shape, dtype) for shape, dtype in kept),
        in_specs=[HBM] * len(operands),
        out_specs=(VM,) * len(kept),
        scratch_shapes=[
            pltpu.VMEM(old.shape, BF16), pltpu.VMEM(mig_send.shape, I32), pltpu.VMEM((nodes // 128, 128), I32),
            pltpu.VMEM(halo_send.shape, I32), pltpu.VMEM(cross_send.shape, I32),
            pltpu.VMEM(lines[0].shape, I32), pltpu.VMEM(lines[0].shape, I32), pltpu.VMEM(lines[0].shape, I32),
            pltpu.VMEM((edges, L), I16),
            pltpu.VMEM((HALF, 2 * L), BF16), pltpu.VMEM((HALF, 2 * L), BF16),
            pltpu.VMEM((mig_send.shape[1], L), BF16), pltpu.VMEM((mig_send.shape[1], L), BF16),
            pltpu.VMEM((far, L), BF16), pltpu.VMEM((far, L), BF16),
            pltpu.SemaphoreType.DMA((9,)), pltpu.SemaphoreType.DMA((len(vectors),)),
            pltpu.SemaphoreType.DMA((steps,)), pltpu.SemaphoreType.DMA((steps,)),
            pltpu.SemaphoreType.DMA((steps + 1,)), pltpu.SemaphoreType.DMA((steps + 1,)),
        ],
        compiler_params=pltpu.CompilerParams(has_side_effects=True, vmem_limit_bytes=24 << 20, **params),
        name="exchange",
    )(*[in_hbm(x) for x in operands])


def layer(parts):
    nodes, edges = parts[0].shape[0], parts[2].shape[0]
    return pl.pallas_call(
        layer_kernel,
        out_shape=(jax.ShapeDtypeStruct((nodes, L), BF16), pltpu.HBM((edges, L), BF16)),
        in_specs=[VM] * len(parts),
        out_specs=(VM, HBM),
        scratch_shapes=[
            pltpu.VMEM((edges, L), BF16),
            pltpu.VMEM((TILE, 2 * L), BF16),
            pltpu.VMEM((TILE, 2 * L), BF16),
            pltpu.VMEM((HALF, 2 * L), F32),
            pltpu.SemaphoreType.DMA((edges // TILE,)),
        ],
        compiler_params=pltpu.CompilerParams(vmem_limit_bytes=24 << 20),
        name="layer",
    )(*parts)


def step(count, node_latent, edge_latent, mig_send, mig_recv, halo_send, cross_send, senders, receivers, edge_live,
         *weights):
    vectors = [w if w.ndim == 2 else w.reshape(1, -1) for w in weights]
    lines = [v.reshape(-1, 128) for v in (senders, receivers, edge_live)]
    return layer(exchange(count, node_latent, mig_send, mig_recv, halo_send, cross_send, lines, edge_latent, vectors))


def solution(mesh):
    rows, line = P(("grp", "dom"), None), P(("grp", "dom"))
    return jax.shard_map(
        functools.partial(step, mesh.shape["dom"]),
        mesh=mesh,
        in_specs=(rows, rows, rows, line, rows, rows, line, line, line) + (P(),) * 12,
        out_specs=(rows, rows),
        check_vma=False,
    )
```

time: 59.3 us -> 28.6 us (0.48)
  the two profiles are of different devices: /device:TPU:32 before, /device:TPU:24 now
where the time goes in v2:
time: 28.6 us; the launch traced here: 28.5 us
  Pallas kernels  27.8 us (97%)
  between operations  0.65 us (2%)
    pallas_call x1, Pallas kernels, exchange(): pl.pallas_call(functools.partial(exchange_kernel, count), out_shape=tuple...  20.2 us
    pallas_call x1, Pallas kernels, layer(): pl.pallas_call(layer_kernel, out_shape=(jax.ShapeDtypeStruct((nodes, L),...  7.57 us

profile of v2, /device:TPU:24, one launch (start us, length us, event | category | flops | bytes accessed | tf_op | source)
XLA Modules:
  0.0 28.5 jit_solution(10961954077397066527)
XLA Ops:
  0.6 20.2 %exchange.1 = (bf16[1024,128]{1,0:T(8,128)(2,1)S(1)}, bf16[256,128]{1,0:T(8,128)(2,1)S(1)}, f32[6144,128]{1,0:T(8,128)S(1)}, s32[6144,128]{1,0:T(8,128)S(1)}, s1...) custom-call(bf16[1024,128]{1,0:T(8,128)(2,1)} %old_hbm.1, ...), custom_call_target="tpu_custom_call" | custom-call | tf_op jit(solution)/shard_map/exchange/pallas_call | solution.py:282
  20.9 7.6 %layer.1 = (bf16[1024,128]{1,0:T(8,128)(2,1)}, bf16[6144,128]{1,0:T(8,128)(2,1)}) custom-call(bf16[1024,128]{1,0:T(8,128)(2,1)S(1)} %get-tuple-element.21.fresh_ref, bf16[256,128]{1,0:T(8,128)(2,1)S(1)} %get-tuple-element.22.far_ref, f32[6144,128]{1,0:T(8,128)S(1)} %get-tuple-element.23.pre_ref, s32[6144,128]{1,0:T(8,128)S(1)} %get-tuple-element.24.words_ref, ...), custom_call_target="tpu_custom_call" | custom-call | tf_op jit(solution)/shard_map/layer/pallas_call | solution.py:306

commit v3 on v2

--- a/solution.py
+++ b/solution.py
@@ -11,12 +11,13 @@
 EPSILON = 1e-05
 L = 128
 HALF = 512
-WORD_TILE = 512
-GATHER_TILE = 1024
-TILE = 1024
+WORD_TILE = 1536
+GATHER_TILE = 3072
+TILE = 3072
 MESH = pl.DeviceIdType.MESH
 F32, BF16, I32, I16 = jnp.float32, jnp.bfloat16, jnp.int32, jnp.int16
 UPPER_S, UPPER_R, LIVE = 30, 29, 28
+EARLY = 6
 
 
 def offset_list():
@@ -55,10 +56,10 @@
 
 def exchange_kernel(count, old_hbm, ms_hbm, mr_hbm, hs_hbm, xs_hbm, snd_hbm, rcv_hbm, live_hbm, edge_hbm, *rest):
     weights_hbm, rest = rest[:12], rest[12:]
-    fresh_ref, far_ref, pre_ref, words_ref, send_ref, rows_ref, edge_ref = rest[:7]
+    fresh_ref, far_ref, pre_ref, send_ref, code_ref, rows_ref, edge_ref = rest[:7]
     weights = rest[7:19]
-    (old_ref, ms_ref, mr_ref, hs_ref, xs_ref, snd_ref, rcv_ref, live_ref, recv_ref, send_tab, recv_tab,
-     leave_buf, arrive_buf, out_buf, in_buf, in_sem, w_sem, lsend, lrecv, hsend, hrecv) = rest[19:]
+    (old_ref, ms_ref, mr_ref, hs_ref, xs_ref, snd_ref, rcv_ref, live_ref, words_ref, recv_ref, send_tab, recv_tab,
+     leave_buf, arrive_buf, out_buf, in_buf, stay_buf, new_buf, via_buf, halo_buf, in_sem, w_sem, lsend, lrecv, hsend, hrecv) = rest[19:]
     shifts = offset_list()
     steps = len(shifts)
     loads = [pltpu.make_async_copy(src, dst, in_sem.at[i]) for i, (src, dst) in enumerate([
@@ -102,47 +103,59 @@
                 device_id={"dom": peers[place]}, device_id_type=MESH))
         return made
 
+    w1e, w1s, w1r = (weights[0].at[pl.ds(i * L, L)] for i in range(3))
+    edges = edge_ref.shape[0]
+    subs = WORD_TILE // 128
+
+    def prepare():
+        for load in loads[2:8]:
+            load.wait()
+        take = jnp.concatenate([down(mr_ref[i:i + 1, :]) for i in range(mr_ref.shape[0])], axis=0).astype(I16)
+        new_hot = one_hot(take, nodes, arrive_buf.shape[0])
+        hwant = jnp.concatenate([down(hs_ref[...]),
+                                 down(jnp.concatenate([xs_ref[...]] * (128 // across), axis=1))[:across]],
+                                axis=0).astype(I16)
+        halo_hot = one_hot(hwant, 0, nodes)
+        stay = dot(one_hot(take, 0, nodes), old_ref[...])
+        new_buf[...] = new_hot
+        via_buf[...] = dot(halo_hot, new_hot).astype(BF16)
+        stay_buf[...] = stay
+        halo_buf[...] = dot(halo_hot, stay.astype(BF16))
+
+        s, r, live = snd_ref[...], rcv_ref[...], live_ref[...]
+        far_s = s >= 2 * HALF
+        s_row = jnp.where(far_s, s - HALF, s & (HALF - 1))
+        s_up = jnp.where(far_s, 0, s >> 9)
+        r_row = r & (HALF - 1)
+        rows_ref[...] = r_row
+        snd_ref[...] = (s_row << 16) | r_row | (s_up << UPPER_S) | ((r >> 9) << UPPER_R) | (live << LIVE)
+        for load in loads[8:11]:
+            load.wait()
+
+        @pl.loop(0, edges // WORD_TILE)
+        def _(step):
+            spot = spot_of(step, WORD_TILE)
+            word = jnp.concatenate([down(snd_ref[pl.ds(step * subs + i, 1), :]) for i in range(subs)], axis=0)
+            words_ref[spot] = word
+            send_ref[spot] = ((word >> 16) & 1023).astype(I16)
+            recv_ref[spot] = (word & 511).astype(I16)
+            code_ref[spot] = (jnp.where((word & (1 << LIVE)) != 0, word & 511, -1 - HALF)
+                              + ((word >> (UPPER_R - 9)) & HALF)).astype(I16)
+            pre_ref[spot] = dot(edge_ref[spot], w1e[...]) + weights[1][...]
+
     if count:
         from_there = [there[steps - 1 - place] for place in range(steps)]
+        early = lax.rem(me, 8) < EARLY
+        pl.when(early)(prepare)
         pl.semaphore_wait(barrier, sum(real.astype(I32) for real in there) + 1)
         first = sends(leave_buf, arrive_buf, moves, lsend, lrecv)
         for copy, real in zip(first, there):
             pl.when(real)(copy.start)
-
-    for load in loads[2:8]:
+        pl.when(jnp.logical_not(early))(prepare)
+    else:
+        prepare()
+    for load in loads[11:]:
         load.wait()
-    take = jnp.concatenate([down(mr_ref[i:i + 1, :]) for i in range(mr_ref.shape[0])], axis=0).astype(I16)
-    stay_hot = one_hot(take, 0, nodes)
-    new_hot = one_hot(take, nodes, arrive_buf.shape[0])
-    hwant = jnp.concatenate([down(hs_ref[...]),
-                             down(jnp.concatenate([xs_ref[...]] * (128 // across), axis=1))[:across]],
-                            axis=0).astype(I16)
-    halo_hot = one_hot(hwant, 0, nodes)
-    via_new = dot(halo_hot, new_hot).astype(BF16)
-    stay = dot(stay_hot, old)
-    halo_stay = dot(halo_hot, stay.astype(BF16))
-
-    s, r, live = snd_ref[...], rcv_ref[...], live_ref[...]
-    far_s = s >= 2 * HALF
-    s_row = jnp.where(far_s, s - HALF, s & (HALF - 1))
-    s_up = jnp.where(far_s, 0, s >> 9)
-    r_row = r & (HALF - 1)
-    rows_ref[...] = r_row
-    snd_ref[...] = (s_row << 16) | r_row | (s_up << UPPER_S) | ((r >> 9) << UPPER_R) | (live << LIVE)
-    for load in loads[8:]:
-        load.wait()
-    w1e, w1s, w1r = weights[0][0:L], weights[0][L:2 * L], weights[0][2 * L:3 * L]
-    edges = edge_ref.shape[0]
-    subs = WORD_TILE // 128
-
-    @pl.loop(0, edges // WORD_TILE)
-    def _(step):
-        spot = spot_of(step, WORD_TILE)
-        word = jnp.concatenate([down(snd_ref[pl.ds(step * subs + i, 1), :]) for i in range(subs)], axis=0)
-        words_ref[spot] = word
-        send_ref[spot] = ((word >> 16) & 1023).astype(I16)
-        recv_ref[spot] = (word & 511).astype(I16)
-        pre_ref[spot] = dot(edge_ref[spot], w1e) + weights[1][...]
 
     if count:
         for copy, real in zip(first, from_there):
@@ -150,7 +163,7 @@
     else:
         arrive_buf[...] = leave_buf[...]
     new = arrive_buf[...]
-    out_buf[...] = (halo_stay + dot(via_new, new)).astype(BF16)
+    out_buf[...] = (halo_buf[...] + dot(via_buf[...], new)).astype(BF16)
     if count:
         second = sends(out_buf, in_buf, halos, hsend, hrecv)
         rows = pl.ds(steps * halos, across)
@@ -162,12 +175,12 @@
             pl.when(real)(copy.start)
         swap.start()
 
-    fresh = (stay + dot(new_hot, new)).astype(BF16)
+    fresh = (stay_buf[...] + dot(new_buf[...], new)).astype(BF16)
     fresh_ref[...] = fresh
-    part = dot(fresh, w1s).astype(BF16)
+    part = dot(fresh, w1s[...]).astype(BF16)
     send_tab[:, 0:L] = part[:HALF]
     send_tab[:, L:2 * L] = part[HALF:]
-    part = dot(fresh, w1r).astype(BF16)
+    part = dot(fresh, w1r[...]).astype(BF16)
     recv_tab[:, 0:L] = part[:HALF]
     recv_tab[:, L:2 * L] = part[HALF:]
 
@@ -190,37 +203,46 @@
         swap.wait()
     else:
         in_buf[...] = out_buf[...]
-    far = dot(in_buf[...], w1s).astype(BF16)
+    far = dot(in_buf[...], w1s[...]).astype(BF16)
     far_ref[...] = jnp.concatenate([far, jnp.zeros((far_ref.shape[0] - far.shape[0], L), BF16)], axis=0)
 
 
-def layer_kernel(fresh_ref, far_ref, pre_ref, words_ref, send_ref, rows_ref, edge_ref,
+def layer_kernel(fresh_ref, far_ref, pre_ref, send_ref, code_ref, rows_ref, edge_ref,
                  ew1_ref, eb1_ref, ew2_ref, eb2_ref, eg_ref, eo_ref,
                  nw1_ref, nb1_ref, nw2_ref, nb2_ref, ng_ref, no_ref,
                  node_out, edge_out, new_buf, side_0, side_1, sums, out_sem):
     edges = edge_ref.shape[0]
     tiles = edges // TILE
     subs = TILE // 128
-    w2 = ew2_ref[...]
+    half = TILE // 2
+    w2 = ew2_ref[...].astype(F32)
+    w2 = (w2 - jnp.mean(w2, axis=-1, keepdims=True)).astype(BF16)
+    b2 = eb2_ref[...] - jnp.mean(eb2_ref[...], axis=-1, keepdims=True)
+    gain = eg_ref[...] * (L ** 0.5)
     nil = jnp.zeros((L, L), BF16)
     w2_pair = jnp.concatenate([jnp.concatenate([w2, nil], axis=1), jnp.concatenate([nil, w2], axis=1)], axis=0)
     sums[...] = jnp.zeros_like(sums)
 
     def messages(tile, side):
         spot = spot_of(tile, TILE)
-        pre = pre_ref[spot] + dot(one_hot(send_ref[spot], HALF, 256), far_ref[...])
-        hidden = jnp.maximum(pre, 0.0).astype(BF16)
-        pair = jnp.concatenate([hidden[:TILE // 2], hidden[TILE // 2:]], axis=1)
-        before = dot(pair, w2_pair)
-        before = jnp.concatenate([before[:, :L], before[:, L:]], axis=0) + eb2_ref[...]
-        message = layer_norm(before, eg_ref[...], eo_ref[...])
-        word = words_ref[spot]
-        kept = jnp.where((word & (1 << LIVE)) != 0, message, 0.0).astype(BF16)
-        new_buf[spot] = (edge_ref[spot].astype(F32) + kept.astype(F32)).astype(BF16)
-        upper = ((word >> 16) & (1 << (UPPER_R - 16))).astype(I16) != jnp.int16(0)
-        zero = jnp.zeros_like(kept)
-        side[:, 0:L] = jnp.where(upper, zero, kept)
-        side[:, L:2 * L] = jnp.where(upper, kept, zero)
+        hot = one_hot(send_ref[spot], HALF, 256)
+        pair = []
+        for i in range(2):
+            part = pre_ref[pl.ds(pl.multiple_of(tile * TILE + i * half, half), half)]
+            part = part + dot(hot[i * half:(i + 1) * half], far_ref[...])
+            pair.append(jnp.maximum(part.astype(BF16), jnp.bfloat16(0)))
+        pair = jnp.concatenate(pair, axis=1)
+        center = jnp.concatenate([dot(pair[:half // 2], w2_pair), dot(pair[half // 2:], w2_pair)], axis=0)
+        center = jnp.concatenate([center[:, :L], center[:, L:]], axis=0) + b2
+        total = jnp.sum(center * center, axis=-1, keepdims=True)
+        message = (center * lax.rsqrt(total + EPSILON * L) * gain + eo_ref[...]).astype(BF16)
+        code = code_ref[spot]
+        zero = jnp.zeros_like(message)
+        kept = jnp.where(code >= jnp.int16(0), message, zero)
+        new_buf[spot] = edge_ref[spot] + kept
+        lower = code < jnp.int16(HALF)
+        side[:, 0:L] = jnp.where(lower, kept, zero)
+        side[:, L:2 * L] = jnp.where(lower, zero, kept)
 
     def save(tile):
         spot = spot_of(tile, TILE)
@@ -233,7 +255,10 @@
             row = jnp.broadcast_to(rows_ref[pl.ds(tile * subs + i, 1), :], (16, 128)).astype(I16)
             row = jnp.concatenate([row] * (HALF // 16), axis=0)
             flat.append(jnp.where(row == below, jnp.bfloat16(1), jnp.bfloat16(0)))
-        sums[...] += dot(jnp.concatenate(flat, axis=1), side[...])
+        flat = jnp.concatenate(flat, axis=1)
+        for i in range(2):
+            rows = slice(i * (HALF // 2), (i + 1) * (HALF // 2))
+            sums[rows] += dot(flat[rows], side[...])
 
     messages(0, side_0)
 
@@ -255,9 +280,13 @@
 
     fresh = fresh_ref[...]
     inbound = jnp.concatenate([sums[:, :L], sums[:, L:]], axis=0).astype(BF16)
-    node_hidden = jnp.maximum(dot(jnp.concatenate([fresh, inbound], axis=1), nw1_ref[...]) + nb1_ref[...], 0.0).astype(BF16)
-    before = dot(node_hidden, nw2_ref[...]) + nb2_ref[...]
-    node_out[...] = (fresh.astype(F32) + layer_norm(before, ng_ref[...], no_ref[...])).astype(BF16)
+    node_in = jnp.concatenate([fresh, inbound], axis=1)
+    half = fresh.shape[0] // 2
+    for i in range(2):
+        rows = slice(i * half, (i + 1) * half)
+        hidden = jnp.maximum(dot(node_in[rows], nw1_ref[...]) + nb1_ref[...], 0.0).astype(BF16)
+        before = dot(hidden, nw2_ref[...]) + nb2_ref[...]
+        node_out[rows] = (fresh[rows].astype(F32) + layer_norm(before, ng_ref[...], no_ref[...])).astype(BF16)
     for tile in range(tiles):
         save(tile).wait()
 
@@ -275,7 +304,7 @@
     nodes, edges = old.shape[0], edge_latent.shape[0]
     far = halo_send.shape[1] + cross_send.shape[1]
     steps = 2 * R
-    kept = [((nodes, L), BF16), ((256, L), BF16), ((edges, L), F32), ((edges, L), I32), ((edges, L), I16),
+    kept = [((nodes, L), BF16), ((256, L), BF16), ((edges, L), F32), ((edges, L), I16), ((edges, L), I16),
             (lines[0].shape, I32), ((edges, L), BF16)] + [(v.shape, v.dtype) for v in vectors]
     operands = [old, mig_send, mig_recv.reshape(-1, 128), halo_send, cross_send, *lines, edge_latent, *vectors]
     params = dict(collective_id=0) if count else {}
@@ -288,10 +317,12 @@
             pltpu.VMEM(old.shape, BF16), pltpu.VMEM(mig_send.shape, I32), pltpu.VMEM((nodes // 128, 128), I32),
             pltpu.VMEM(halo_send.shape, I32), pltpu.VMEM(cross_send.shape, I32),
             pltpu.VMEM(lines[0].shape, I32), pltpu.VMEM(lines[0].shape, I32), pltpu.VMEM(lines[0].shape, I32),
-            pltpu.VMEM((edges, L), I16),
+            pltpu.VMEM((edges, L), I32), pltpu.VMEM((edges, L), I16),
             pltpu.VMEM((HALF, 2 * L), BF16), pltpu.VMEM((HALF, 2 * L), BF16),
             pltpu.VMEM((mig_send.shape[1], L), BF16), pltpu.VMEM((mig_send.shape[1], L), BF16),
             pltpu.VMEM((far, L), BF16), pltpu.VMEM((far, L), BF16),
+            pltpu.VMEM((nodes, L), F32), pltpu.VMEM((nodes, mig_send.shape[1]), BF16),
+            pltpu.VMEM((far, mig_send.shape[1]), BF16), pltpu.VMEM((far, L), F32),
             pltpu.SemaphoreType.DMA((9,)), pltpu.SemaphoreType.DMA((len(vectors),)),
             pltpu.SemaphoreType.DMA((steps,)), pltpu.SemaphoreType.DMA((steps,)),
             pltpu.SemaphoreType.DMA((steps + 1,)), pltpu.SemaphoreType.DMA((steps + 1,)),

time: 28.6 us -> 26.3 us (0.920)
  Pallas kernels: 27.8 us -> 25.6 us
    pallas_call x1, Pallas kernels: 7.57 us -> 5.43 us  [layer(): pl.pallas_call(layer_kernel, out_shape=(jax.ShapeDtypeStruct((nodes, L),...]
where the time goes in v3:
time: 26.3 us; the launch traced here: 26.2 us
  Pallas kernels  25.6 us (97%)
  between operations  0.65 us (2%)
    pallas_call x1, Pallas kernels, exchange(): pl.pallas_call(functools.partial(exchange_kernel, count), out_shape=tuple...  20.2 us
    pallas_call x1, Pallas kernels, layer(): pl.pallas_call(layer_kernel, out_shape=(jax.ShapeDtypeStruct((nodes, L),...  5.43 us

profile of v3, /device:TPU:24, one launch (start us, length us, event | category | flops | bytes accessed | tf_op | source)
XLA Modules:
  0.0 26.2 jit_solution(15598643316891667818)
XLA Ops:
  0.6 20.2 %exchange.1 = (bf16[1024,128]{1,0:T(8,128)(2,1)S(1)}, bf16[256,128]{1,0:T(8,128)(2,1)S(1)}, f32[6144,128]{1,0:T(8,128)S(1)}, s16[6144,128]{1,0:T(8,128)(2,1)S(1)...) custom-call(bf16[1024,128]{1,0:T(8,128)(2,1)} %old_hbm.1, ...), custom_call_target="tpu_custom_call" | custom-call | tf_op jit(solution)/shard_map/exchange/pallas_call | solution.py:311
  20.8 5.4 %layer.1 = (bf16[1024,128]{1,0:T(8,128)(2,1)}, bf16[6144,128]{1,0:T(8,128)(2,1)}) custom-call(bf16[1024,128]{1,0:T(8,128)(2,1)S(1)} %get-tuple-element.21.fresh_ref, bf16[256,128]{1,0:T(8,128)(2,1)S(1)} %get-tuple-element.22.far_ref, f32[6144,128]{1,0:T(8,128)S(1)} %get-tuple-element.23.pre_ref, s16[6144,128]{1,0:T(8,128)(2,1)S(1)} %get-tuple-element.24.send_ref, ...), custom_call_target="tpu_custom_call" | custom-call | tf_op jit(solution)/shard_map/layer/pallas_call | solution.py:337

commit v4 on v3

--- a/solution.py
+++ b/solution.py
@@ -59,7 +59,8 @@
     fresh_ref, far_ref, pre_ref, send_ref, code_ref, rows_ref, edge_ref = rest[:7]
     weights = rest[7:19]
     (old_ref, ms_ref, mr_ref, hs_ref, xs_ref, snd_ref, rcv_ref, live_ref, words_ref, recv_ref, send_tab, recv_tab,
-     leave_buf, arrive_buf, out_buf, in_buf, stay_buf, new_buf, via_buf, halo_buf, in_sem, w_sem, lsend, lrecv, hsend, hrecv) = rest[19:]
+     leave_buf, arrive_buf, out_buf, in_buf, stay_buf, new_buf, via_buf, halo_buf, beside_buf, pick_buf, pick_in,
+     in_sem, w_sem, lsend, lrecv, hsend, hrecv, bsend, brecv, psend, precv) = rest[19:]
     shifts = offset_list()
     steps = len(shifts)
     loads = [pltpu.make_async_copy(src, dst, in_sem.at[i]) for i, (src, dst) in enumerate([
@@ -69,6 +70,8 @@
 
     arrive_buf[...] = jnp.zeros_like(arrive_buf)
     in_buf[...] = jnp.zeros_like(in_buf)
+    beside_buf[...] = jnp.zeros_like(beside_buf)
+    pick_in[...] = jnp.zeros_like(pick_in)
     if count:
         me = lax.axis_index("dom")
         other = 1 - lax.axis_index("grp")
@@ -106,9 +109,10 @@
     w1e, w1s, w1r = (weights[0].at[pl.ds(i * L, L)] for i in range(3))
     edges = edge_ref.shape[0]
     subs = WORD_TILE // 128
-
-    def prepare():
-        for load in loads[2:8]:
+    ahead_rows, behind_rows = pl.ds(0, 2 * moves), pl.ds(2 * moves, 2 * moves)
+
+    def plan_rows():
+        for load in loads[2:5]:
             load.wait()
         take = jnp.concatenate([down(mr_ref[i:i + 1, :]) for i in range(mr_ref.shape[0])], axis=0).astype(I16)
         new_hot = one_hot(take, nodes, arrive_buf.shape[0])
@@ -118,10 +122,16 @@
         halo_hot = one_hot(hwant, 0, nodes)
         stay = dot(one_hot(take, 0, nodes), old_ref[...])
         new_buf[...] = new_hot
-        via_buf[...] = dot(halo_hot, new_hot).astype(BF16)
+        via = dot(halo_hot, new_hot).astype(BF16)
+        via_buf[...] = via
+        pick_buf[0:2 * halos] = via[0:2 * halos, 2 * moves:]
+        pick_buf[2 * halos:4 * halos] = via[2 * halos:4 * halos, :2 * moves]
         stay_buf[...] = stay
         halo_buf[...] = dot(halo_hot, stay.astype(BF16))
 
+    def plan_edges():
+        for load in loads[5:8]:
+            load.wait()
         s, r, live = snd_ref[...], rcv_ref[...], live_ref[...]
         far_s = s >= 2 * HALF
         s_row = jnp.where(far_s, s - HALF, s & (HALF - 1))
@@ -143,37 +153,74 @@
                               + ((word >> (UPPER_R - 9)) & HALF)).astype(I16)
             pre_ref[spot] = dot(edge_ref[spot], w1e[...]) + weights[1][...]
 
+    def start(copies, conditions):
+        for copy, real in zip(copies, conditions):
+            pl.when(real)(copy.start)
+
+    def arrived(copies, conditions):
+        for copy, real in zip(copies, conditions):
+            pl.when(real)(copy.wait_recv)
+
     if count:
         from_there = [there[steps - 1 - place] for place in range(steps)]
+        before_us, after_us = there[R - 1], there[R]
         early = lax.rem(me, 8) < EARLY
-        pl.when(early)(prepare)
+
+        @pl.when(early)
+        def _():
+            plan_rows()
+            plan_edges()
+
         pl.semaphore_wait(barrier, sum(real.astype(I32) for real in there) + 1)
         first = sends(leave_buf, arrive_buf, moves, lsend, lrecv)
-        for copy, real in zip(first, there):
-            pl.when(real)(copy.start)
-        pl.when(jnp.logical_not(early))(prepare)
-    else:
-        prepare()
-    for load in loads[11:]:
-        load.wait()
-
-    if count:
-        for copy, real in zip(first, from_there):
-            pl.when(real)(copy.wait_recv)
-    else:
-        arrive_buf[...] = leave_buf[...]
-    new = arrive_buf[...]
-    out_buf[...] = (halo_buf[...] + dot(via_buf[...], new)).astype(BF16)
-    if count:
+        start(first, there)
+        shared = []
+        for place in range(steps):
+            rows = pl.ds(place * moves, moves)
+            shared.append(pltpu.make_async_remote_copy(
+                src_ref=leave_buf.at[rows], dst_ref=beside_buf.at[rows],
+                send_sem=bsend.at[place], recv_sem=brecv.at[place],
+                device_id={"dom": peers[R - 1] if place % 2 == 0 else peers[R]}, device_id_type=MESH))
+        shared_to = [before_us, after_us] * R
+        shared_from = [after_us, before_us] * R
+        start(shared, shared_to)
+
+        @pl.when(jnp.logical_not(early))
+        def _():
+            plan_rows()
+
+        picks = sends(pick_buf, pick_in, halos, psend, precv)
+        start(picks, there)
         second = sends(out_buf, in_buf, halos, hsend, hrecv)
         rows = pl.ds(steps * halos, across)
         swap = pltpu.make_async_remote_copy(
             src_ref=out_buf.at[rows], dst_ref=in_buf.at[rows],
             send_sem=hsend.at[steps], recv_sem=hrecv.at[steps],
             device_id={"grp": other}, device_id_type=MESH)
-        for copy, real in zip(second, there):
-            pl.when(real)(copy.start)
+
+        arrived(first[R:], from_there[R:])
+        slots = pl.ds(2 * halos, 2 * halos)
+        out_buf[slots] = (halo_buf[slots] + dot(via_buf[slots, 2 * moves:], arrive_buf[behind_rows])).astype(BF16)
+        start(second[R:], there[R:])
+
+        @pl.when(jnp.logical_not(early))
+        def _():
+            plan_edges()
+
+        arrived(first[:R], from_there[:R])
+        slots = pl.ds(0, 2 * halos)
+        out_buf[slots] = (halo_buf[slots] + dot(via_buf[slots, :2 * moves], arrive_buf[ahead_rows])).astype(BF16)
+        start(second[:R], there[:R])
+        out_buf[rows] = (halo_buf[rows] + dot(via_buf[rows], arrive_buf[...])).astype(BF16)
         swap.start()
+    else:
+        plan_rows()
+        plan_edges()
+        arrive_buf[...] = leave_buf[...]
+        out_buf[...] = (halo_buf[...] + dot(via_buf[...], arrive_buf[...])).astype(BF16)
+    for load in loads[11:]:
+        load.wait()
+    new = arrive_buf[...]
 
     fresh = (stay_buf[...] + dot(new_buf[...], new)).astype(BF16)
     fresh_ref[...] = fresh
@@ -194,16 +241,27 @@
                          + jnp.where((word & (1 << UPPER_R)) != 0, got_r[:, L:], got_r[:, :L]))
 
     if count:
-        for copy, real in zip(first, there):
-            pl.when(real)(copy.wait_send)
-        for copy, real in zip(second, there):
-            pl.when(real)(copy.wait_send)
-        for copy, real in zip(second, from_there):
-            pl.when(real)(copy.wait_recv)
+        for copies, conditions in ((first, there), (shared, shared_to), (picks, there), (second, there)):
+            for copy, real in zip(copies, conditions):
+                pl.when(real)(copy.wait_send)
+        arrived(shared, shared_from)
+        arrived(picks, from_there)
+        arrived(second, from_there)
         swap.wait()
+
+        def list_of(buf, place):
+            return buf[place * moves:(place + 1) * moves]
+
+        filled = []
+        for place, (one, two) in enumerate((((beside_buf, 2), (leave_buf, 3)), ((leave_buf, 2), (beside_buf, 3)),
+                                            ((beside_buf, 0), (leave_buf, 1)), ((leave_buf, 0), (beside_buf, 1)))):
+            rows = pl.ds(place * halos, halos)
+            table = jnp.concatenate([list_of(*one), list_of(*two)], axis=0)
+            filled.append((in_buf[rows].astype(F32) + dot(pick_in[rows], table)).astype(BF16))
+        halo = jnp.concatenate(filled + [in_buf[pl.ds(steps * halos, across)]], axis=0)
     else:
-        in_buf[...] = out_buf[...]
-    far = dot(in_buf[...], w1s[...]).astype(BF16)
+        halo = out_buf[...]
+    far = dot(halo, w1s[...]).astype(BF16)
     far_ref[...] = jnp.concatenate([far, jnp.zeros((far_ref.shape[0] - far.shape[0], L), BF16)], axis=0)
 
 
@@ -323,9 +381,12 @@
             pltpu.VMEM((far, L), BF16), pltpu.VMEM((far, L), BF16),
             pltpu.VMEM((nodes, L), F32), pltpu.VMEM((nodes, mig_send.shape[1]), BF16),
             pltpu.VMEM((far, mig_send.shape[1]), BF16), pltpu.VMEM((far, L), F32),
+            pltpu.VMEM((mig_send.shape[1], L), BF16), pltpu.VMEM((halo_send.shape[1], 128), BF16),
+            pltpu.VMEM((halo_send.shape[1], 128), BF16),
             pltpu.SemaphoreType.DMA((9,)), pltpu.SemaphoreType.DMA((len(vectors),)),
             pltpu.SemaphoreType.DMA((steps,)), pltpu.SemaphoreType.DMA((steps,)),
             pltpu.SemaphoreType.DMA((steps + 1,)), pltpu.SemaphoreType.DMA((steps + 1,)),
+            *[pltpu.SemaphoreType.DMA((steps,))] * 4,
         ],
         compiler_params=pltpu.CompilerParams(has_side_effects=True, vmem_limit_bytes=24 << 20, **params),
         name="exchange",

time: 26.3 us -> 25.9 us (0.985)
  Pallas kernels: 25.6 us -> 25.1 us
    pallas_call x1, Pallas kernels: 20.2 us -> 19.7 us  [exchange(): pl.pallas_call(functools.partial(exchange_kernel, count), out_shape=tuple...]
where the time goes in v4:
time: 25.9 us; the launch traced here: 25.8 us
  Pallas kernels  25.1 us (97%)
  between operations  0.65 us (3%)
    pallas_call x1, Pallas kernels, exchange(): pl.pallas_call(functools.partial(exchange_kernel, count), out_shape=tuple...  19.7 us
    pallas_call x1, Pallas kernels, layer(): pl.pallas_call(layer_kernel, out_shape=(jax.ShapeDtypeStruct((nodes, L),...  5.42 us

profile of v4, /device:TPU:24, one launch (start us, length us, event | category | flops | bytes accessed | tf_op | source)
XLA Modules:
  0.0 25.8 jit_solution(3507127377562604155)
XLA Ops:
  0.6 19.7 %exchange.1 = (bf16[1024,128]{1,0:T(8,128)(2,1)S(1)}, bf16[256,128]{1,0:T(8,128)(2,1)S(1)}, f32[6144,128]{1,0:T(8,128)S(1)}, s16[6144,128]{1,0:T(8,128)(2,1)S(1)...) custom-call(bf16[1024,128]{1,0:T(8,128)(2,1)} %old_hbm.1, ...), custom_call_target="tpu_custom_call" | custom-call | tf_op jit(solution)/shard_map/exchange/pallas_call | solution.py:369
  20.4 5.4 %layer.1 = (bf16[1024,128]{1,0:T(8,128)(2,1)}, bf16[6144,128]{1,0:T(8,128)(2,1)}) custom-call(bf16[1024,128]{1,0:T(8,128)(2,1)S(1)} %get-tuple-element.21.fresh_ref, bf16[256,128]{1,0:T(8,128)(2,1)S(1)} %get-tuple-element.22.far_ref, f32[6144,128]{1,0:T(8,128)S(1)} %get-tuple-element.23.pre_ref, s16[6144,128]{1,0:T(8,128)(2,1)S(1)} %get-tuple-element.24.send_ref, ...), custom_call_target="tpu_custom_call" | custom-call | tf_op jit(solution)/shard_map/layer/pallas_call | solution.py:398

commit v5 on v4

--- a/solution.py
+++ b/solution.py
@@ -11,13 +11,14 @@
 EPSILON = 1e-05
 L = 128
 HALF = 512
-WORD_TILE = 1536
+WORD_TILE = 3072
 GATHER_TILE = 3072
-TILE = 3072
+SIZES = (1536, 1536, 1536, 1536)
 MESH = pl.DeviceIdType.MESH
 F32, BF16, I32, I16 = jnp.float32, jnp.bfloat16, jnp.int32, jnp.int16
-UPPER_S, UPPER_R, LIVE = 30, 29, 28
-EARLY = 6
+UPPER_S, UPPER_R, DEAD = 30, 9, 15
+EARLY = 4
+PIECES = 2
 
 
 def offset_list():
@@ -56,11 +57,11 @@
 
 def exchange_kernel(count, old_hbm, ms_hbm, mr_hbm, hs_hbm, xs_hbm, snd_hbm, rcv_hbm, live_hbm, edge_hbm, *rest):
     weights_hbm, rest = rest[:12], rest[12:]
-    fresh_ref, far_ref, pre_ref, send_ref, code_ref, rows_ref, edge_ref = rest[:7]
-    weights = rest[7:19]
-    (old_ref, ms_ref, mr_ref, hs_ref, xs_ref, snd_ref, rcv_ref, live_ref, words_ref, recv_ref, send_tab, recv_tab,
+    fresh_ref, far_ref, pre_ref, words_ref, rows_ref, edge_ref = rest[:6]
+    weights = rest[6:18]
+    (old_ref, ms_ref, mr_ref, hs_ref, xs_ref, snd_ref, rcv_ref, live_ref, send_tab, recv_tab,
      leave_buf, arrive_buf, out_buf, in_buf, stay_buf, new_buf, via_buf, halo_buf, beside_buf, pick_buf, pick_in,
-     in_sem, w_sem, lsend, lrecv, hsend, hrecv, bsend, brecv, psend, precv) = rest[19:]
+     in_sem, w_sem, lsend, lrecv, hsend, hrecv, bsend, brecv, psend, precv) = rest[18:]
     shifts = offset_list()
     steps = len(shifts)
     loads = [pltpu.make_async_copy(src, dst, in_sem.at[i]) for i, (src, dst) in enumerate([
@@ -136,21 +137,15 @@
         far_s = s >= 2 * HALF
         s_row = jnp.where(far_s, s - HALF, s & (HALF - 1))
         s_up = jnp.where(far_s, 0, s >> 9)
-        r_row = r & (HALF - 1)
-        rows_ref[...] = r_row
-        snd_ref[...] = (s_row << 16) | r_row | (s_up << UPPER_S) | ((r >> 9) << UPPER_R) | (live << LIVE)
+        rows_ref[...] = r & (HALF - 1)
+        snd_ref[...] = (s_up << UPPER_S) | (s_row << 16) | ((1 - live) << DEAD) | r
         for load in loads[8:11]:
             load.wait()
 
         @pl.loop(0, edges // WORD_TILE)
         def _(step):
             spot = spot_of(step, WORD_TILE)
-            word = jnp.concatenate([down(snd_ref[pl.ds(step * subs + i, 1), :]) for i in range(subs)], axis=0)
-            words_ref[spot] = word
-            send_ref[spot] = ((word >> 16) & 1023).astype(I16)
-            recv_ref[spot] = (word & 511).astype(I16)
-            code_ref[spot] = (jnp.where((word & (1 << LIVE)) != 0, word & 511, -1 - HALF)
-                              + ((word >> (UPPER_R - 9)) & HALF)).astype(I16)
+            words_ref[spot] = jnp.concatenate([down(snd_ref[pl.ds(step * subs + i, 1), :]) for i in range(subs)], axis=0)
             pre_ref[spot] = dot(edge_ref[spot], w1e[...]) + weights[1][...]
 
     def start(copies, conditions):
@@ -234,9 +229,9 @@
     @pl.loop(0, edges // GATHER_TILE)
     def _(step):
         spot = spot_of(step, GATHER_TILE)
-        got_s = dot(one_hot(send_ref[spot], 0, HALF), send_tab[...])
-        got_r = dot(one_hot(recv_ref[spot], 0, HALF), recv_tab[...])
         word = words_ref[spot]
+        got_s = dot(one_hot(((word >> 16) & 1023).astype(I16), 0, HALF), send_tab[...])
+        got_r = dot(one_hot((word & (HALF - 1)).astype(I16), 0, HALF), recv_tab[...])
         pre_ref[spot] = (pre_ref[spot] + jnp.where((word & (1 << UPPER_S)) != 0, got_s[:, L:], got_s[:, :L])
                          + jnp.where((word & (1 << UPPER_R)) != 0, got_r[:, L:], got_r[:, :L]))
 
@@ -265,14 +260,11 @@
     far_ref[...] = jnp.concatenate([far, jnp.zeros((far_ref.shape[0] - far.shape[0], L), BF16)], axis=0)
 
 
-def layer_kernel(fresh_ref, far_ref, pre_ref, send_ref, code_ref, rows_ref, edge_ref,
+def layer_kernel(fresh_ref, far_ref, pre_ref, words_ref, rows_ref, edge_ref,
                  ew1_ref, eb1_ref, ew2_ref, eb2_ref, eg_ref, eo_ref,
                  nw1_ref, nb1_ref, nw2_ref, nb2_ref, ng_ref, no_ref,
-                 node_out, edge_out, new_buf, side_0, side_1, sums, out_sem):
-    edges = edge_ref.shape[0]
-    tiles = edges // TILE
-    subs = TILE // 128
-    half = TILE // 2
+                 node_out, edge_out, new_buf, node_buf, side_0, side_1, sums, out_sem, node_sem):
+    tiles = [(sum(SIZES[:i]), size) for i, size in enumerate(SIZES)]
     w2 = ew2_ref[...].astype(F32)
     w2 = (w2 - jnp.mean(w2, axis=-1, keepdims=True)).astype(BF16)
     b2 = eb2_ref[...] - jnp.mean(eb2_ref[...], axis=-1, keepdims=True)
@@ -282,71 +274,73 @@
     sums[...] = jnp.zeros_like(sums)
 
     def messages(tile, side):
-        spot = spot_of(tile, TILE)
-        hot = one_hot(send_ref[spot], HALF, 256)
+        first, size = tiles[tile]
+        half = size // 2
+        spot = pl.ds(first, size)
+        word = words_ref[spot]
+        far_slot = (word >> 16).astype(I16)
         pair = []
         for i in range(2):
-            part = pre_ref[pl.ds(pl.multiple_of(tile * TILE + i * half, half), half)]
-            part = part + dot(hot[i * half:(i + 1) * half], far_ref[...])
+            part = pre_ref[pl.ds(first + i * half, half)]
+            part = part + dot(one_hot(far_slot[i * half:(i + 1) * half], HALF, 256), far_ref[...])
             pair.append(jnp.maximum(part.astype(BF16), jnp.bfloat16(0)))
         pair = jnp.concatenate(pair, axis=1)
         center = jnp.concatenate([dot(pair[:half // 2], w2_pair), dot(pair[half // 2:], w2_pair)], axis=0)
         center = jnp.concatenate([center[:, :L], center[:, L:]], axis=0) + b2
         total = jnp.sum(center * center, axis=-1, keepdims=True)
         message = (center * lax.rsqrt(total + EPSILON * L) * gain + eo_ref[...]).astype(BF16)
-        code = code_ref[spot]
+        code = word.astype(I16)
         zero = jnp.zeros_like(message)
         kept = jnp.where(code >= jnp.int16(0), message, zero)
         new_buf[spot] = edge_ref[spot] + kept
         lower = code < jnp.int16(HALF)
-        side[:, 0:L] = jnp.where(lower, kept, zero)
-        side[:, L:2 * L] = jnp.where(lower, zero, kept)
+        side[0:size, 0:L] = jnp.where(lower, kept, zero)
+        side[0:size, L:2 * L] = jnp.where(lower, zero, kept)
 
     def save(tile):
-        spot = spot_of(tile, TILE)
+        spot = pl.ds(*tiles[tile])
         return pltpu.make_async_copy(new_buf.at[spot], edge_out.at[spot], out_sem.at[tile])
 
     def gather_in(tile, side):
+        first, size = tiles[tile]
         below = lax.broadcasted_iota(I32, (HALF, 128), 0).astype(I16)
         flat = []
-        for i in range(subs):
-            row = jnp.broadcast_to(rows_ref[pl.ds(tile * subs + i, 1), :], (16, 128)).astype(I16)
+        for i in range(first // 128, (first + size) // 128):
+            row = jnp.broadcast_to(rows_ref[i:i + 1, :], (16, 128)).astype(I16)
             row = jnp.concatenate([row] * (HALF // 16), axis=0)
             flat.append(jnp.where(row == below, jnp.bfloat16(1), jnp.bfloat16(0)))
         flat = jnp.concatenate(flat, axis=1)
         for i in range(2):
             rows = slice(i * (HALF // 2), (i + 1) * (HALF // 2))
-            sums[rows] += dot(flat[rows], side[...])
-
+            sums[rows] += dot(flat[rows], side[0:size])
+
+    sides = (side_0, side_1)
     messages(0, side_0)
-
-    @pl.loop(0, tiles // 2 - 1)
-    def _(step):
-        tile = 2 * step
+    for tile in range(len(tiles)):
+        if tile + 1 < len(tiles):
+            messages(tile + 1, sides[(tile + 1) % 2])
+        gather_in(tile, sides[tile % 2])
         save(tile).start()
-        gather_in(tile, side_0)
-        messages(tile + 1, side_1)
-        save(tile + 1).start()
-        gather_in(tile + 1, side_1)
-        messages(tile + 2, side_0)
-
-    save(tiles - 2).start()
-    gather_in(tiles - 2, side_0)
-    messages(tiles - 1, side_1)
-    save(tiles - 1).start()
-    gather_in(tiles - 1, side_1)
 
     fresh = fresh_ref[...]
     inbound = jnp.concatenate([sums[:, :L], sums[:, L:]], axis=0).astype(BF16)
     node_in = jnp.concatenate([fresh, inbound], axis=1)
-    half = fresh.shape[0] // 2
-    for i in range(2):
-        rows = slice(i * half, (i + 1) * half)
+    piece = fresh.shape[0] // PIECES
+    stores = []
+    for i in range(PIECES):
+        rows = slice(i * piece, (i + 1) * piece)
         hidden = jnp.maximum(dot(node_in[rows], nw1_ref[...]) + nb1_ref[...], 0.0).astype(BF16)
         before = dot(hidden, nw2_ref[...]) + nb2_ref[...]
-        node_out[rows] = (fresh[rows].astype(F32) + layer_norm(before, ng_ref[...], no_ref[...])).astype(BF16)
-    for tile in range(tiles):
+        node_buf[rows] = (fresh[rows].astype(F32) + layer_norm(before, ng_ref[...], no_ref[...])).astype(BF16)
+        stores.append(pltpu.make_async_copy(node_buf.at[pl.ds(i * piece, piece)], node_out.at[pl.ds(i * piece, piece)],
+                                            node_sem.at[i]))
+        if i:
+            stores[i - 1].start()
+    stores[-1].start()
+    for tile in range(len(tiles)):
         save(tile).wait()
+    for store in stores:
+        store.wait()
 
 
 VM = pl.BlockSpec(memory_space=pltpu.VMEM)
@@ -362,7 +356,7 @@
     nodes, edges = old.shape[0], edge_latent.shape[0]
     far = halo_send.shape[1] + cross_send.shape[1]
     steps = 2 * R
-    kept = [((nodes, L), BF16), ((256, L), BF16), ((edges, L), F32), ((edges, L), I16), ((edges, L), I16),
+    kept = [((nodes, L), BF16), ((256, L), BF16), ((edges, L), F32), ((edges, L), I32),
             (lines[0].shape, I32), ((edges, L), BF16)] + [(v.shape, v.dtype) for v in vectors]
     operands = [old, mig_send, mig_recv.reshape(-1, 128), halo_send, cross_send, *lines, edge_latent, *vectors]
     params = dict(collective_id=0) if count else {}
@@ -375,7 +369,6 @@
             pltpu.VMEM(old.shape, BF16), pltpu.VMEM(mig_send.shape, I32), pltpu.VMEM((nodes // 128, 128), I32),
             pltpu.VMEM(halo_send.shape, I32), pltpu.VMEM(cross_send.shape, I32),
             pltpu.VMEM(lines[0].shape, I32), pltpu.VMEM(lines[0].shape, I32), pltpu.VMEM(lines[0].shape, I32),
-            pltpu.VMEM((edges, L), I32), pltpu.VMEM((edges, L), I16),
             pltpu.VMEM((HALF, 2 * L), BF16), pltpu.VMEM((HALF, 2 * L), BF16),
             pltpu.VMEM((mig_send.shape[1], L), BF16), pltpu.VMEM((mig_send.shape[1], L), BF16),
             pltpu.VMEM((far, L), BF16), pltpu.VMEM((far, L), BF16),
@@ -397,15 +390,17 @@
     nodes, edges = parts[0].shape[0], parts[2].shape[0]
     return pl.pallas_call(
         layer_kernel,
-        out_shape=(jax.ShapeDtypeStruct((nodes, L), BF16), pltpu.HBM((edges, L), BF16)),
+        out_shape=(pltpu.HBM((nodes, L), BF16), pltpu.HBM((edges, L), BF16)),
         in_specs=[VM] * len(parts),
-        out_specs=(VM, HBM),
+        out_specs=(HBM, HBM),
         scratch_shapes=[
             pltpu.VMEM((edges, L), BF16),
-            pltpu.VMEM((TILE, 2 * L), BF16),
-            pltpu.VMEM((TILE, 2 * L), BF16),
+            pltpu.VMEM((nodes, L), BF16),
+            pltpu.VMEM((max(SIZES), 2 * L), BF16),
+            pltpu.VMEM((max(SIZES), 2 * L), BF16),
             pltpu.VMEM((HALF, 2 * L), F32),
-            pltpu.SemaphoreType.DMA((edges // TILE,)),
+            pltpu.SemaphoreType.DMA((len(SIZES),)),
+            pltpu.SemaphoreType.DMA((PIECES,)),
         ],
         compiler_params=pltpu.CompilerParams(vmem_limit_bytes=24 << 20),
         name="layer",

time: 25.9 us -> 24 us (0.927)
  Pallas kernels: 25.1 us -> 23.2 us
    pallas_call x1, Pallas kernels: 19.7 us -> 17.9 us  [exchange(): pl.pallas_call(functools.partial(exchange_kernel, count), out_shape=tuple...]
where the time goes in v5:
time: 24 us; the launch traced here: 23.9 us
  Pallas kernels  23.2 us (97%)
  between operations  0.65 us (3%)
    pallas_call x1, Pallas kernels, exchange(): pl.pallas_call(functools.partial(exchange_kernel, count), out_shape=tuple...  17.9 us
    pallas_call x1, Pallas kernels, layer(): pl.pallas_call(layer_kernel, out_shape=(pltpu.HBM((nodes, L), BF16), pltp...  5.33 us

profile of v5, /device:TPU:24, one launch (start us, length us, event | category | flops | bytes accessed | tf_op | source)
XLA Modules:
  0.0 23.9 jit_solution(2518506494938037445)
XLA Ops:
  0.6 17.9 %exchange.1 = (bf16[1024,128]{1,0:T(8,128)(2,1)S(1)}, bf16[256,128]{1,0:T(8,128)(2,1)S(1)}, f32[6144,128]{1,0:T(8,128)S(1)}, s32[6144,128]{1,0:T(8,128)S(1)}, s3...) custom-call(bf16[1024,128]{1,0:T(8,128)(2,1)} %old_hbm.1, ...), custom_call_target="tpu_custom_call" | custom-call | tf_op jit(solution)/shard_map/exchange/pallas_call | solution.py:363
  18.5 5.3 %layer.1 = (bf16[1024,128]{1,0:T(8,128)(2,1)}, bf16[6144,128]{1,0:T(8,128)(2,1)}) custom-call(bf16[1024,128]{1,0:T(8,128)(2,1)S(1)} %get-tuple-element.20.fresh_ref, bf16[256,128]{1,0:T(8,128)(2,1)S(1)} %get-tuple-element.21.far_ref, f32[6144,128]{1,0:T(8,128)S(1)} %get-tuple-element.22.pre_ref, s32[6144,128]{1,0:T(8,128)S(1)} %get-tuple-element.23.words_ref, ...), custom_call_target="tpu_custom_call" | custom-call | tf_op jit(solution)/shard_map/layer/pallas_call | solution.py:391

commit v6 on v5

--- a/solution.py
+++ b/solution.py
@@ -18,6 +18,7 @@
 F32, BF16, I32, I16 = jnp.float32, jnp.bfloat16, jnp.int32, jnp.int16
 UPPER_S, UPPER_R, DEAD = 30, 9, 15
 EARLY = 4
+LOCAL_DEEP = False
 PIECES = 2
 
 
@@ -60,7 +61,7 @@
     fresh_ref, far_ref, pre_ref, words_ref, rows_ref, edge_ref = rest[:6]
     weights = rest[6:18]
     (old_ref, ms_ref, mr_ref, hs_ref, xs_ref, snd_ref, rcv_ref, live_ref, send_tab, recv_tab,
-     leave_buf, arrive_buf, out_buf, in_buf, stay_buf, new_buf, via_buf, halo_buf, beside_buf, pick_buf, pick_in,
+     leave_buf, arrive_buf, out_buf, in_buf, stay_buf, new_buf, via_buf, halo_buf, beside_buf, pick_buf, pick_in, fill_tab, rank_tab, rank_ref, late_tab,
      in_sem, w_sem, lsend, lrecv, hsend, hrecv, bsend, brecv, psend, precv) = rest[18:]
     shifts = offset_list()
     steps = len(shifts)
@@ -73,6 +74,7 @@
     in_buf[...] = jnp.zeros_like(in_buf)
     beside_buf[...] = jnp.zeros_like(beside_buf)
     pick_in[...] = jnp.zeros_like(pick_in)
+    far_ref[...] = jnp.zeros_like(far_ref)
     if count:
         me = lax.axis_index("dom")
         other = 1 - lax.axis_index("grp")
@@ -123,6 +125,9 @@
         halo_hot = one_hot(hwant, 0, nodes)
         stay = dot(one_hot(take, 0, nodes), old_ref[...])
         new_buf[...] = new_hot
+        rank = jnp.where(take >= jnp.int16(nodes), take - jnp.int16(nodes - 1), jnp.int16(0)).astype(F32).astype(BF16)
+        rank_tab[:, 0:L] = rank[:HALF]
+        rank_tab[:, L:2 * L] = rank[HALF:]
         via = dot(halo_hot, new_hot).astype(BF16)
         via_buf[...] = via
         pick_buf[0:2 * halos] = via[0:2 * halos, 2 * moves:]
@@ -148,6 +153,53 @@
             words_ref[spot] = jnp.concatenate([down(snd_ref[pl.ds(step * subs + i, 1), :]) for i in range(subs)], axis=0)
             pre_ref[spot] = dot(edge_ref[spot], w1e[...]) + weights[1][...]
 
+    def project(rows):
+        for tab, w in ((send_tab, w1s), (recv_tab, w1r)):
+            part = dot(rows, w[...]).astype(BF16)
+            tab[:, 0:L] = part[:HALF]
+            tab[:, L:2 * L] = part[HALF:]
+
+    def pick_half(word, bit, got):
+        return jnp.where((word & (1 << bit)) != 0, got[:, L:], got[:, :L])
+
+    def hot_pair(word):
+        return (one_hot(((word >> 16) & 1023).astype(I16), 0, HALF), one_hot((word & (HALF - 1)).astype(I16), 0, HALF))
+
+    def gather_old(step):
+        spot = pl.ds(step * GATHER_TILE, GATHER_TILE)
+        word = words_ref[spot]
+        hot_s, hot_r = hot_pair(word)
+        pre_ref[spot] = (pre_ref[spot] + pick_half(word, UPPER_S, dot(hot_s, send_tab[...]))
+                         + pick_half(word, UPPER_R, dot(hot_r, recv_tab[...])))
+        rank_s = pick_half(word, UPPER_S, dot(hot_s, rank_tab[...])).astype(I32)
+        rank_r = pick_half(word, UPPER_R, dot(hot_r, rank_tab[...])).astype(I32)
+        rank_ref[spot] = (rank_r << 16) | rank_s
+
+    def gather_new():
+        late_tab[0:steps * moves] = dot(arrive_buf[...], w1s[...]).astype(BF16)
+        late_tab[steps * moves:] = dot(arrive_buf[...], w1r[...]).astype(BF16)
+
+        @pl.loop(0, edges // GATHER_TILE)
+        def _(step):
+            spot = spot_of(step, GATHER_TILE)
+            word = rank_ref[spot]
+            hot = jnp.concatenate([one_hot(word.astype(I16), 1, steps * moves),
+                                   one_hot((word >> 16).astype(I16), 1, steps * moves)], axis=1)
+            mid = GATHER_TILE // 2
+            pre_ref[spot] = pre_ref[spot] + jnp.concatenate([dot(hot[:mid], late_tab[...]), dot(hot[mid:], late_tab[...])],
+                                                            axis=0)
+
+    def gather_all(fresh):
+        project(fresh)
+
+        @pl.loop(0, edges // GATHER_TILE)
+        def _(step):
+            spot = spot_of(step, GATHER_TILE)
+            word = words_ref[spot]
+            hot_s, hot_r = hot_pair(word)
+            pre_ref[spot] = (pre_ref[spot] + pick_half(word, UPPER_S, dot(hot_s, send_tab[...]))
+                             + pick_half(word, UPPER_R, dot(hot_r, recv_tab[...])))
+
     def start(copies, conditions):
         for copy, real in zip(copies, conditions):
             pl.when(real)(copy.start)
@@ -165,6 +217,13 @@
         def _():
             plan_rows()
             plan_edges()
+
+        deep = (lax.rem(me, 32) < 2) & (me >= 32)
+
+        @pl.when(deep)
+        def _():
+            project(stay_buf[...].astype(BF16))
+            gather_old(0)
 
         pl.semaphore_wait(barrier, sum(real.astype(I32) for real in there) + 1)
         first = sends(leave_buf, arrive_buf, moves, lsend, lrecv)
@@ -186,6 +245,12 @@
 
         picks = sends(pick_buf, pick_in, halos, psend, precv)
         start(picks, there)
+
+        @pl.when(deep)
+        def _():
+            for step in range(1, edges // GATHER_TILE):
+                gather_old(step)
+
         second = sends(out_buf, in_buf, halos, hsend, hrecv)
         rows = pl.ds(steps * halos, across)
         swap = pltpu.make_async_remote_copy(
@@ -193,24 +258,38 @@
             send_sem=hsend.at[steps], recv_sem=hrecv.at[steps],
             device_id={"grp": other}, device_id_type=MESH)
 
-        arrived(first[R:], from_there[R:])
-        slots = pl.ds(2 * halos, 2 * halos)
-        out_buf[slots] = (halo_buf[slots] + dot(via_buf[slots, 2 * moves:], arrive_buf[behind_rows])).astype(BF16)
-        start(second[R:], there[R:])
+        def send_ahead():
+            arrived(first[R:], from_there[R:])
+            slots = pl.ds(2 * halos, 2 * halos)
+            out_buf[slots] = (halo_buf[slots] + dot(via_buf[slots, 2 * moves:], arrive_buf[behind_rows])).astype(BF16)
+            start(second[R:], there[R:])
+
+        def send_behind():
+            arrived(first[:R], from_there[:R])
+            slots = pl.ds(0, 2 * halos)
+            out_buf[slots] = (halo_buf[slots] + dot(via_buf[slots, :2 * moves], arrive_buf[ahead_rows])).astype(BF16)
+            start(second[:R], there[:R])
+
+        @pl.when(early)
+        def _():
+            send_behind()
+            send_ahead()
 
         @pl.when(jnp.logical_not(early))
         def _():
+            send_ahead()
             plan_edges()
-
-        arrived(first[:R], from_there[:R])
-        slots = pl.ds(0, 2 * halos)
-        out_buf[slots] = (halo_buf[slots] + dot(via_buf[slots, :2 * moves], arrive_buf[ahead_rows])).astype(BF16)
-        start(second[:R], there[:R])
+            send_behind()
+
         out_buf[rows] = (halo_buf[rows] + dot(via_buf[rows], arrive_buf[...])).astype(BF16)
         swap.start()
     else:
         plan_rows()
         plan_edges()
+        if LOCAL_DEEP:
+            project(stay_buf[...].astype(BF16))
+            for step in range(edges // GATHER_TILE):
+                gather_old(step)
         arrive_buf[...] = leave_buf[...]
         out_buf[...] = (halo_buf[...] + dot(via_buf[...], arrive_buf[...])).astype(BF16)
     for load in loads[11:]:
@@ -219,45 +298,41 @@
 
     fresh = (stay_buf[...] + dot(new_buf[...], new)).astype(BF16)
     fresh_ref[...] = fresh
-    part = dot(fresh, w1s[...]).astype(BF16)
-    send_tab[:, 0:L] = part[:HALF]
-    send_tab[:, L:2 * L] = part[HALF:]
-    part = dot(fresh, w1r[...]).astype(BF16)
-    recv_tab[:, 0:L] = part[:HALF]
-    recv_tab[:, L:2 * L] = part[HALF:]
-
-    @pl.loop(0, edges // GATHER_TILE)
-    def _(step):
-        spot = spot_of(step, GATHER_TILE)
-        word = words_ref[spot]
-        got_s = dot(one_hot(((word >> 16) & 1023).astype(I16), 0, HALF), send_tab[...])
-        got_r = dot(one_hot((word & (HALF - 1)).astype(I16), 0, HALF), recv_tab[...])
-        pre_ref[spot] = (pre_ref[spot] + jnp.where((word & (1 << UPPER_S)) != 0, got_s[:, L:], got_s[:, :L])
-                         + jnp.where((word & (1 << UPPER_R)) != 0, got_r[:, L:], got_r[:, :L]))
-
     if count:
+        arrived(shared, shared_from)
+
+        def list_of(buf, place):
+            return buf[place * moves:(place + 1) * moves]
+
+        for place, (one, two) in enumerate((((beside_buf, 2), (leave_buf, 3)), ((leave_buf, 2), (beside_buf, 3)),
+                                            ((beside_buf, 0), (leave_buf, 1)), ((leave_buf, 0), (beside_buf, 1)))):
+            table = jnp.concatenate([list_of(*one), list_of(*two)], axis=0)
+            fill_tab[place, 0:L] = w1s[...]
+            fill_tab[place, L:2 * L] = dot(table, w1s[...]).astype(BF16)
+
+    if count:
+        pl.when(deep)(gather_new)
+        pl.when(jnp.logical_not(deep))(lambda: gather_all(fresh_ref[...]))
+    elif LOCAL_DEEP:
+        gather_new()
+    else:
+        gather_all(fresh)
+
+    tail = pl.ds(steps * halos, across)
+    if count:
+        arrived(picks, from_there)
+        arrived(second, from_there)
+        swap.wait_recv()
+        for place in range(steps):
+            rows = pl.ds(place * halos, halos)
+            far_ref[rows] = dot(jnp.concatenate([in_buf[rows], pick_in[rows]], axis=1), fill_tab[place]).astype(BF16)
+        far_ref[tail] = dot(in_buf[tail], w1s[...]).astype(BF16)
+        swap.wait_send()
         for copies, conditions in ((first, there), (shared, shared_to), (picks, there), (second, there)):
             for copy, real in zip(copies, conditions):
                 pl.when(real)(copy.wait_send)
-        arrived(shared, shared_from)
-        arrived(picks, from_there)
-        arrived(second, from_there)
-        swap.wait()
-
-        def list_of(buf, place):
-            return buf[place * moves:(place + 1) * moves]
-
-        filled = []
-        for place, (one, two) in enumerate((((beside_buf, 2), (leave_buf, 3)), ((leave_buf, 2), (beside_buf, 3)),
-                                            ((beside_buf, 0), (leave_buf, 1)), ((leave_buf, 0), (beside_buf, 1)))):
-            rows = pl.ds(place * halos, halos)
-            table = jnp.concatenate([list_of(*one), list_of(*two)], axis=0)
-            filled.append((in_buf[rows].astype(F32) + dot(pick_in[rows], table)).astype(BF16))
-        halo = jnp.concatenate(filled + [in_buf[pl.ds(steps * halos, across)]], axis=0)
     else:
-        halo = out_buf[...]
-    far = dot(halo, w1s[...]).astype(BF16)
-    far_ref[...] = jnp.concatenate([far, jnp.zeros((far_ref.shape[0] - far.shape[0], L), BF16)], axis=0)
+        far_ref[pl.ds(0, steps * halos + across)] = dot(out_buf[...], w1s[...]).astype(BF16)
 
 
 def layer_kernel(fresh_ref, far_ref, pre_ref, words_ref, rows_ref, edge_ref,
@@ -376,6 +451,8 @@
             pltpu.VMEM((far, mig_send.shape[1]), BF16), pltpu.VMEM((far, L), F32),
             pltpu.VMEM((mig_send.shape[1], L), BF16), pltpu.VMEM((halo_send.shape[1], 128), BF16),
             pltpu.VMEM((halo_send.shape[1], 128), BF16),
+            pltpu.VMEM((steps, 2 * L, L), BF16), pltpu.VMEM((HALF, 2 * L), BF16), pltpu.VMEM((edges, L), I32),
+            pltpu.VMEM((2 * mig_send.shape[1], L), BF16),
             pltpu.SemaphoreType.DMA((9,)), pltpu.SemaphoreType.DMA((len(vectors),)),
             pltpu.SemaphoreType.DMA((steps,)), pltpu.SemaphoreType.DMA((steps,)),
             pltpu.SemaphoreType.DMA((steps + 1,)), pltpu.SemaphoreType.DMA((steps + 1,)),

time: 24 us -> 22.6 us (0.942)
  Pallas kernels: 23.2 us -> 21.7 us
    pallas_call x1, Pallas kernels: 17.9 us -> 16.4 us  [exchange(): pl.pallas_call(functools.partial(exchange_kernel, count), out_shape=tuple...]
where the time goes in v6:
time: 22.6 us; the launch traced here: 22.5 us
  Pallas kernels  21.7 us (96%)
  between operations  0.81 us (4%)
    pallas_call x1, Pallas kernels, exchange(): pl.pallas_call(functools.partial(exchange_kernel, count), out_shape=tuple...  16.4 us
    pallas_call x1, Pallas kernels, layer(): pl.pallas_call(layer_kernel, out_shape=(pltpu.HBM((nodes, L), BF16), pltp...  5.33 us

profile of v6, /device:TPU:24, one launch (start us, length us, event | category | flops | bytes accessed | tf_op | source)
XLA Modules:
  0.0 22.5 jit_solution(14950930923539598497)
XLA Ops:
  0.6 16.4 %exchange.1 = (bf16[1024,128]{1,0:T(8,128)(2,1)S(1)}, bf16[256,128]{1,0:T(8,128)(2,1)S(1)}, f32[6144,128]{1,0:T(8,128)S(1)}, s32[6144,128]{1,0:T(8,128)S(1)}, s3...) custom-call(bf16[1024,128]{1,0:T(8,128)(2,1)} %old_hbm.1, ...), custom_call_target="tpu_custom_call" | custom-call | tf_op jit(solution)/shard_map/exchange/pallas_call | solution.py:438
  17.1 5.3 %layer.1 = (bf16[1024,128]{1,0:T(8,128)(2,1)}, bf16[6144,128]{1,0:T(8,128)(2,1)}) custom-call(bf16[1024,128]{1,0:T(8,128)(2,1)S(1)} %get-tuple-element.20.fresh_ref, bf16[256,128]{1,0:T(8,128)(2,1)S(1)} %get-tuple-element.21.far_ref, f32[6144,128]{1,0:T(8,128)S(1)} %get-tuple-element.22.pre_ref, s32[6144,128]{1,0:T(8,128)S(1)} %get-tuple-element.23.words_ref, ...), custom_call_target="tpu_custom_call" | custom-call | tf_op jit(solution)/shard_map/layer/pallas_call | solution.py:468
